TPU v7x, 256 devices: a whole 4x4x8 slice. The times are simulated.
256 devices in a mesh: grp: 4 (over x), rep: 8 (over y, z_hi), tp: 8 (over z_lo, core).
Axes of the slice: x: 4, y: 4, z: 8 (z_hi: 2, z_lo: 4; z = z_hi * 4 + z_lo), core: 2. Of those that a mesh axis runs over, the one named last changes fastest.
Arguments:
- noise_in: bfloat16 [1024, 3072], P('rep', 'tp'), may hold values from -6 to 6
- noise_renoise: bfloat16 [1024, 3072], P('rep', 'tp'), may hold values from -6 to 6
- text_cond: bfloat16 [8, 3072], P('rep'), may hold values from -3 to 3
- t_index: int32 [8], P('rep'), may hold values from 0 to 999
- gains: float32 [3, 3072], replicated, may hold values from 0.5 to 1.5
- up_weights: bfloat16 [3, 3072, 12288], P(None, 'rep', 'tp'), may hold values from -0.109375 to 0.109375
- down_weights: bfloat16 [3, 12288, 3072], P(None, 'tp', 'rep'), may hold values from -0.0546875 to 0.0546875
Outputs:
- generated: bfloat16 [1024, 3072], P('rep', 'tp')
- up_grads: float32 [4, 3072, 12288], P('grp', 'rep', 'tp')
- down_grads: float32 [4, 12288, 3072], P('grp', 'tp', 'rep')
All inputs are finite; a program needn't handle non-finite values. Where the computation divides by a largest or mean magnitude, that divisor is 1e-20 or more.
Results may differ from a plain program's by a relative error of at most 0.01.
Values may be sent and summed in bfloat16 or wider, within the bound.
A program may use at most 128 MiB of HBM per device.

v0:
```python
import math

import jax
import jax.numpy as jnp
from jax import lax
from jax.sharding import PartitionSpec as P

IMG_TOK = 128


def split_up(shard, dim, count):
    before, after = (shard.shape[:dim], shard.shape[dim + 1 :])
    return jnp.moveaxis(shard.reshape(*before, count, -1, *after), dim, 0)


def sum_at_owner(shard, axis, dim):
    count = lax.axis_size(axis)
    blocks = lax.all_to_all(split_up(shard, dim, count), axis, 0, 0, tiled=True)
    return jnp.sum(blocks, axis=0)


def rows_first(arrays, axis, dims):
    turned = [jnp.moveaxis(a, dim, 0) for a, dim in zip(arrays, dims)]
    widths = [t[0].size for t in turned]
    both = jnp.concatenate([t.reshape(-1, w) for t, w in zip(turned, widths)], axis=1)
    out = lax.all_gather(both, axis, axis=0, tiled=True)
    blocks = jnp.split(out, [sum(widths[:k]) for k in range(1, len(widths))], axis=1)
    return tuple(
        (
            jnp.moveaxis(b.reshape(-1, *t.shape[1:]), 0, dim)
            for b, t, dim in zip(blocks, turned, dims)
        )
    )


def swapped(shard, axis, stride):
    return lax.ppermute(shard, axis, [(i, i ^ 1 << stride) for i in range(lax.axis_size(axis))])


def sent_to_all(shard, axis):
    copies = jnp.broadcast_to(shard, (lax.axis_size(axis), *shard.shape))
    return lax.all_to_all(copies, axis, split_axis=0, concat_axis=0, tiled=True)


def of_everyone(shard, axis):
    everything = sent_to_all(shard, axis)
    return jnp.sum(everything, axis=0)


def packed_total(arrays, axis):
    ends = [0]
    for a in arrays:
        ends.append(ends[-1] + a.size)
    subtotal = of_everyone(jnp.concatenate([a.ravel() for a in arrays]), axis)
    return tuple((subtotal[b:e].reshape(a.shape) for a, b, e in zip(arrays, ends, ends[1:])))


def gelu_tanh(value):
    return jax.nn.gelu(value, approximate=True)


def normalize(whole_rows, own_gain, cond_part):
    values = whole_rows.astype(jnp.float32)
    factor = lax.rsqrt(jnp.mean(values * values, axis=-1, keepdims=True) + 1e-06)
    return (values * factor * own_gain[None, :] * (1.0 + cond_part)).astype(jnp.bfloat16)


def front_pass(inputs, own_gain, cond_part, up_full, down_full, active):
    whole_rows = lax.all_gather(inputs, "tp", axis=1, tiled=True)
    normed = normalize(whole_rows, own_gain, cond_part)
    row_count = normed.shape[0]

    def front_compute():
        hidden_pre = jnp.dot(normed, up_full, preferred_element_type=jnp.float32)
        hidden = gelu_tanh(hidden_pre).astype(jnp.bfloat16)
        return (hidden_pre, hidden, jnp.dot(hidden, down_full, preferred_element_type=jnp.float32))

    def front_skipped():
        return (
            jnp.zeros((row_count, up_full.shape[1]), jnp.float32),
            jnp.zeros((row_count, up_full.shape[1]), jnp.bfloat16),
            jnp.zeros((row_count, down_full.shape[1]), jnp.float32),
        )

    hidden_pre, hidden, partial_terms = lax.cond(active, front_compute, front_skipped)
    summed = sum_at_owner(partial_terms, "tp", 1)
    return (normed, hidden_pre, hidden, summed)


def pre_gradient(upstream, hidden_pre, down_full, active):

    def pre_compute():
        hidden_grad = jnp.dot(upstream, down_full.T, preferred_element_type=jnp.float32)
        return jax.vjp(gelu_tanh, hidden_pre)[1](hidden_grad)[0].astype(jnp.bfloat16)

    def pre_skipped():
        return jnp.zeros(hidden_pre.shape, jnp.bfloat16)

    return lax.cond(active, pre_compute, pre_skipped)


def in_order(half_index, mine_part, other_part):
    first_part = jnp.where(half_index == 0, mine_part, other_part)
    second_part = jnp.where(half_index == 0, other_part, mine_part)
    return jnp.concatenate([first_part, second_part], axis=0)


def padded(half_index, mine_part):
    return in_order(half_index, mine_part, jnp.zeros_like(mine_part))


def body(noise_in, noise_renoise, text_cond, t_index, gains, up_weights, down_weights):
    group_index = lax.axis_index("grp")
    model_index = jnp.maximum(group_index - 1, 0)
    half_index = group_index % 2
    is_student = group_index < 2
    is_teacher = group_index == 2
    is_fake = group_index == 3
    own_up = lax.dynamic_index_in_dim(up_weights, model_index, 0, keepdims=False)
    own_down = lax.dynamic_index_in_dim(down_weights, model_index, 0, keepdims=False)
    up_full, down_full = rows_first((own_up, own_down), "rep", (0, 1))
    own_gain = lax.dynamic_index_in_dim(gains, model_index, 0, keepdims=False)
    cond_rows = jnp.repeat(text_cond.astype(jnp.float32), IMG_TOK, axis=0)
    row_count = noise_in.shape[0]
    half_rows = row_count // 2
    row_start = half_index * half_rows
    student_in = lax.dynamic_slice_in_dim(noise_in, row_start, half_rows, 0)
    cond_half = lax.dynamic_slice_in_dim(cond_rows, row_start, half_rows, 0)
    normed_s, pre_s, hidden_s, summed_s = front_pass(
        student_in, own_gain, cond_half, up_full, down_full, is_student
    )
    own_half = (student_in.astype(jnp.float32) + summed_s).astype(jnp.bfloat16)
    across = swapped(own_half, "grp", 1)
    mine_half = jnp.where(is_student, own_half, across)
    other_half = swapped(mine_half, "grp", 0)
    generated = in_order(half_index, mine_half, other_half)
    sigma = 0.1 + 0.8 * t_index.astype(jnp.float32) / 999.0
    sigma_rows = jnp.repeat(sigma, IMG_TOK)[:, None]
    noised = (
        (1.0 - sigma_rows) * generated.astype(jnp.float32)
        + sigma_rows * noise_renoise.astype(jnp.float32)
    ).astype(jnp.bfloat16)
    normed_c, pre_c, hidden_c, summed_c = front_pass(
        noised, own_gain, cond_rows, up_full, down_full, jnp.logical_not(is_student)
    )
    predicted = (noised.astype(jnp.float32) + summed_c).astype(jnp.bfloat16).astype(jnp.float32)
    nothing = jnp.zeros_like(predicted)
    real_f, fake_f = packed_total(
        (jnp.where(is_teacher, predicted, nothing), jnp.where(is_fake, predicted, nothing)), "grp"
    )
    gen_f = generated.astype(jnp.float32)
    images = t_index.shape[0]
    distances = jnp.sum(jnp.abs(gen_f - real_f).reshape(images, IMG_TOK, -1), axis=(1, 2))
    distances = of_everyone(distances, "tp")
    width_all = gen_f.shape[1] * lax.axis_size("tp")
    image_norm = distances / (IMG_TOK * width_all) + 1e-05
    tokens_all = row_count * lax.axis_size("rep")
    push_scale = 1.0 / math.sqrt(tokens_all)
    student_push = (
        (fake_f - real_f) / jnp.repeat(image_norm, IMG_TOK)[:, None] * push_scale
    ).astype(jnp.bfloat16)
    fake_push = ((fake_f - gen_f) * push_scale).astype(jnp.bfloat16)
    push_half = lax.dynamic_slice_in_dim(student_push, row_start, half_rows, 0)
    upstream_s = lax.all_gather(push_half, "tp", axis=1, tiled=True)
    pre_grad_s = pre_gradient(upstream_s, pre_s, down_full, is_student)
    upstream_c = lax.all_gather(fake_push, "tp", axis=1, tiled=True)
    pre_grad_c = pre_gradient(upstream_c, pre_c, down_full, is_fake)
    normed = jnp.where(is_student, padded(half_index, normed_s), normed_c)
    upstream = jnp.where(is_student, padded(half_index, upstream_s), upstream_c)
    hidden = jnp.where(is_student, padded(half_index, hidden_s), hidden_c)
    pre_grad = jnp.where(is_student, padded(half_index, pre_grad_s), pre_grad_c)
    normed_cols, upstream_cols = (
        lax.all_to_all(normed, "rep", split_axis=1, concat_axis=0, tiled=True),
        lax.all_to_all(upstream, "rep", split_axis=1, concat_axis=0, tiled=True),
    )
    hidden_all, pre_grad_all = (
        lax.all_gather(hidden, "rep", axis=0, tiled=True),
        lax.all_gather(pre_grad, "rep", axis=0, tiled=True),
    )

    def weight_grads():
        up_grad = jnp.dot(normed_cols.T, pre_grad_all, preferred_element_type=jnp.float32)
        down_grad = jnp.dot(hidden_all.T, upstream_cols, preferred_element_type=jnp.float32)
        return (up_grad, down_grad)

    def no_grads():
        return (
            jnp.zeros((normed_cols.shape[1], pre_grad_all.shape[1]), jnp.float32),
            jnp.zeros((hidden_all.shape[1], upstream_cols.shape[1]), jnp.float32),
        )

    up_grad, down_grad = lax.cond(jnp.logical_not(is_teacher), weight_grads, no_grads)
    return (generated, up_grad[None], down_grad[None])


def solution(mesh):
    in_specs = (
        P("rep", "tp"),
        P("rep", "tp"),
        P("rep", None),
        P("rep"),
        P(),
        P(None, "rep", "tp"),
        P(None, "tp", "rep"),
    )
    out_specs = (P("rep", "tp"), P("grp", "rep", "tp"), P("grp", "tp", "rep"))
    return jax.shard_map(body, mesh=mesh, in_specs=in_specs, out_specs=out_specs, check_vma=False)
```

profile of v0, /device:TPU:102, one launch (start us, length us, event | category | flops | bytes accessed | tf_op | source)
XLA Modules:
  0.0 693.3 jit_solution(5607220857907933052)
XLA Ops:
  7.2 1.9 copy-done
  9.2 1.1 constant_dynamic-slice_fusion
  10.3 1.6 copy.36
  11.9 1.4 dynamic-slice_bitcast_fusion
  13.2 1.7 pad_maximum_fusion
  15.0 0.8 copy-done.8
  15.9 14.6 %all_gather.21 = bf16[64,3072]{1,0:T(8,128)(2,1)S(1)} all-gather(bf16[64,384]{1,0:T(8,128)(2,1)S(1)} %constant_dynamic-slice_fusion.2), channel_id=1, replica_groups=mesh['grp'=4,'rep'=8,'tp'=8] {'tp'}, dimensions={1}, use_global_device_ids=true | all-gather | bytes 442368 | tf_op jit(solution)/shard_map/all_gather | solution.py:69
  30.7 0.8 constant_dynamic-slice_fusion.1
  31.8 306.0 %all-gather.4.cloned.1.call-done = bf16[3072,3072]{1,0:T(8,128)(2,1)} async-done(((bf16[384,3072]{1,0:T(8,128)(2,1)}), bf16[3072,3072]{1,0:T(8,128)(2,1)}) %all-gather.4.cloned.1.call-update) | async-done | bytes 18874384 | tf_op jit(solution)/shard_map/all_gather | solution.py:26
  337.8 16.4 %fusion.49 = (bf16[3072,1536]{1,0:T(8,128)(2,1)}, bf16[1536,3072]{0,1:T(8,128)(2,1)}, bf16[3072,1536]{1,0:T(8,128)(2,1)}) fusion(bf16[3072,3072]{1,0:T(8,128)(2,1)} %all-gather.4.cloned.1.call-done), kind=kLoop, calls=%fused_computation.95 | loop fusion | bytes 47185920 | tf_op jit(solution)/shard_map/split | solution.py:27
  354.2 0.8 conditional.5
  355.3 40.6 %all_to_all.60 = f32[8,64,384]{2,1,0:T(8,128)S(1)} all-to-all(f32[8,64,384]{2,1,0:T(8,128)S(1)} %copy.38), channel_id=1, replica_groups=mesh['grp'=4,'rep'=8,'tp'=8] {'tp'}, dimensions={0} | all-to-all | bytes 1572864 | tf_op jit(solution)/shard_map/all_to_all | solution.py:18
  395.9 13.6 %collective-permute-start = (bf16[64,384]{1,0:T(8,128)(2,1)S(1)}, bf16[64,384]{1,0:T(8,128)(2,1)S(1)}, u32[]{:S(2)}, u32[]{:S(2)}) collective-permute-start(bf16[64,384]{1,0:T(8,128)(2,1)S(1)} %add_convert_fusion.1), channel_id=1, source_target_pairs={{0,128},{64,192},{128,0},{192,64},{1,129},{65,193},{129,1},{193,65... | collective-permute-start | bytes 147464 | tf_op jit(solution)/shard_map/ppermute | solution.py:37
  409.6 2.1 collective-permute-done
  412.4 3.4 collective-permute-done.1
  416.5 15.8 %all_gather.23 = bf16[128,3072]{1,0:T(8,128)(2,1)S(1)} all-gather(bf16[128,384]{1,0:T(8,128)(2,1)S(1)} %get-tuple-element.111), channel_id=1, replica_groups=mesh['grp'=4,'rep'=8,'tp'=8] {'tp'}, dimensions={1}, use_global_device_ids=true | all-gather | bytes 884736 | tf_op jit(solution)/shard_map/all_gather | solution.py:69
  432.6 1.3 maximum_select_fusion
  433.9 13.0 %conditional.6 = (f32[128,1536]{1,0:T(8,128)S(1)}, bf16[128,1536]{1,0:T(8,128)(2,1)}, f32[128,3072]{1,0:T(8,128)S(1)}) conditional(s32[]{:T(128)} %convert_element_type.88, () %tuple.52, (bf16[128,3072]{1,0:T(8,128)(2,1)S(1)}, bf16[3072,1536]{1,0:T(8,128)(2,1)}, bf16[1536,3072]{0,1:T(8,128)(2,1)}) %tuple.53), branch_computations={%region_5.6_spmd, %region_6.7_spmd} | conditional | flops 2417688576 | bytes 22806552 | solution.py:85
  433.9 6.1 fusion.15
  440.0 6.9 %fusion.52 = f32[128,3072]{1,0:T(8,128)S(1)} fusion(bf16[128,1536]{1,0:T(8,128)(2,1)} %get-tuple-element.144, bf16[1536,3072]{0,1:T(8,128)(2,1)} %get-tuple-element.106), kind=kOutput, calls=%fused_computation.98 | convolution fusion | flops 1207959552 | bytes 11403264 | tf_op jit(solution)/shard_map/cond/branch_1_fun/dot_general | solution.py:76
  446.9 0.9 copy-done.5
  448.3 1.6 copy.42
  449.9 6.0 all-to-all-start.2
  455.9 1.0 broadcast_select_fusion.5
  456.9 1.9 maximum_select_fusion.3
  458.7 40.8 %all-to-all-done.2 = f32[8,128,384]{2,1,0:T(8,128)S(1)} async-done(((f32[8,128,384]{2,1,0:T(8,128)}), f32[8,128,384]{2,1,0:T(8,128)S(1)}, u32[]{:S(2)}, u32[]{:S(2)}) %all-to-all-start.2) | async-done | bytes 1572896 | tf_op jit(solution)/shard_map/all_to_all | solution.py:18
  499.7 2.0 broadcast_in_dim.31
  501.7 4.5 all-to-all-start.3
  506.2 18.9 %all-to-all-done.3 = f32[4,1,98304]{2,1,0:T(1,128)S(1)} async-done(((f32[4,1,98304]{2,1,0:T(1,128)}), f32[4,1,98304]{2,1,0:T(1,128)S(1)}, u32[]{:S(2)}, u32[]{:S(2)}) %all-to-all-start.3) | async-done | bytes 1572896 | tf_op jit(solution)/shard_map/all_to_all | solution.py:42
  525.1 1.4 reduce_sum.67
  527.4 1.2 broadcast_in_dim.32
  528.6 5.3 all-to-all-start.4
  533.9 16.8 %all_gather.25 = bf16[128,3072]{1,0:T(8,128)(2,1)S(1)} all-gather(bf16[128,384]{1,0:T(8,128)(2,1)S(1)} %get-tuple-element.131), channel_id=1, replica_groups=mesh['grp'=4,'rep'=8,'tp'=8] {'tp'}, dimensions={1}, use_global_device_ids=true | all-gather | bytes 884736 | tf_op jit(solution)/shard_map/all_gather | solution.py:166
  550.7 5.5 conditional.8
  550.7 5.5 fusion.29
  557.5 14.5 %all_gather.24 = bf16[64,3072]{1,0:T(8,128)(2,1)S(1)} all-gather(bf16[64,384]{1,0:T(8,128)(2,1)S(1)} %fusion.46), channel_id=1, replica_groups=mesh['grp'=4,'rep'=8,'tp'=8] {'tp'}, dimensions={1}, use_global_device_ids=true | all-gather | bytes 442368 | tf_op jit(solution)/shard_map/all_gather | solution.py:164
  572.1 0.8 maximum_select_fusion.2
  573.3 1.0 copy.58
  574.3 5.3 all-to-all-start.1
  579.8 1.0 copy.57
  580.8 31.2 %all-to-all-done.1 = bf16[128,8,384]{2,0,1:T(8,128)(2,1)S(1)} async-done(((bf16[128,8,384]{2,0,1:T(8,128)(2,1)}), bf16[128,8,384]{2,0,1:T(8,128)(2,1)S(1)}, u32[]{:S(2)}, u32[]{:S(2)}) %all-to-all-start.1) | async-done | bytes 786464 | tf_op jit(solution)/shard_map/all_to_all | solution.py:173
  612.0 3.5 all-to-all-start.5
  615.6 22.0 %all-to-all-done.5 = bf16[128,8,384]{2,0,1:T(8,128)(2,1)S(1)} async-done(((bf16[128,8,384]{2,0,1:T(8,128)(2,1)}), bf16[128,8,384]{2,0,1:T(8,128)(2,1)S(1)}, u32[]{:S(2)}, u32[]{:S(2)}) %all-to-all-start.5) | async-done | bytes 786464 | tf_op jit(solution)/shard_map/all_to_all | solution.py:174
  637.6 39.0 %all-gather.6.cloned.1.call-done = bf16[1024,1536]{1,0:T(8,128)(2,1)} async-done(((bf16[128,1536]{1,0:T(8,128)(2,1)}), bf16[1024,1536]{1,0:T(8,128)(2,1)}) %all-gather.6.cloned.1.call-update) | async-done | bytes 3145744 | tf_op jit(solution)/shard_map/all_gather | solution.py:178
  676.6 8.1 %conditional.9 = (f32[1,384,1536]{2,1,0:T(8,128)}, f32[1,1536,384]{2,1,0:T(8,128)}) conditional(s32[]{:T(128)} %convert_element_type.80, () %tuple.50, (bf16[8,128,384]{2,1,0:T(8,128)(2,1)S(1)}, bf16[1024,1536]{1,0:T(8,128)(2,1)}, bf16[8,128,384]{2,1,0:T(8,128)(2,1)S(1)}, bf16[1024,1536]{1,0:T(8,128)(2,1)}) %tuple.100), branch_computations={%region_15.16_spmd, %region_16.17_spmd} | conditional | flops 2415919104 | bytes 25165868 | solution.py:192
  676.6 5.3 convolution_bitcast_fusion
  681.9 2.8 convolution_bitcast_fusion.1
  684.7 2.0 copy-done.1
  (64 shorter events, 5.6 us)
Async XLA Ops:
  7.2 2.0 copy-start
  7.2 330.6 %all-gather.4.cloned.1.call-start = ((), (), s32[]{:S(2)}) async-start(), calls=%async_computation.6 | async-start | bytes 21233664 | tf_op jit(solution)/shard_map/all_gather | solution.py:26
  15.0 0.9 copy-start.8
  15.0 16.5 %copy-start.10 = (bf16[1,3072]{1,0:T(2,128)(2,1)S(1)}, bf16[1,3072]{1,0:T(2,128)(2,1)}, u32[]{:S(2)}) copy-start(bf16[1,3072]{1,0:T(2,128)(2,1)} %param.19) | copy-start | bytes 18436
  355.1 60.7 %copy-start.9 = (bf16[128,384]{1,0:T(8,128)(2,1)S(1)}, bf16[128,384]{1,0:T(8,128)(2,1)}, u32[]{:S(2)}) copy-start(bf16[128,384]{1,0:T(8,128)(2,1)} %param.18) | copy-start | bytes 294916
  395.9 15.7 %collective-permute-start = (bf16[64,384]{1,0:T(8,128)(2,1)S(1)}, bf16[64,384]{1,0:T(8,128)(2,1)S(1)}, u32[]{:S(2)}, u32[]{:S(2)}) collective-permute-start(bf16[64,384]{1,0:T(8,128)(2,1)S(1)} %add_convert_fusion.1), channel_id=1, source_target_pairs={{0,128},{64,192},{128,0},{192,64},{1,129},{65,193},{129,1},{193,65... | collective-permute-start | bytes 147464 | tf_op jit(solution)/shard_map/ppermute | solution.py:37
  411.6 4.2 collective-permute-start.1
  416.5 16.1 %copy-start.3 = (bf16[128,384]{1,0:T(8,128)(2,1)}, bf16[128,384]{1,0:T(8,128)(2,1)S(1)}, u32[]{:S(2)}) copy-start(bf16[128,384]{1,0:T(8,128)(2,1)S(1)} %get-tuple-element.111) | copy-start | bytes 294916
  446.9 0.9 copy-start.5
  449.9 49.6 %all-to-all-start.2 = ((f32[8,128,384]{2,1,0:T(8,128)}), f32[8,128,384]{2,1,0:T(8,128)S(1)}, u32[]{:S(2)}, u32[]{:S(2)}) async-start(f32[8,128,384]{2,1,0:T(8,128)} %copy.42), calls=%async_computation.2 | async-start | bytes 3145728 | tf_op jit(solution)/shard_map/all_to_all | solution.py:18
  455.9 43.8 %copy-start.4 = (bf16[128,384]{1,0:T(8,128)(2,1)S(1)}, bf16[128,384]{1,0:T(8,128)(2,1)}, u32[]{:S(2)}) copy-start(bf16[128,384]{1,0:T(8,128)(2,1)} %copy-done.3) | copy-start | bytes 294916
  455.9 181.7 %all-gather.8.cloned.1.call-start = ((), (), s32[]{:S(2)}) async-start(), calls=%async_computation.8 | async-start | bytes 3538944 | tf_op jit(solution)/shard_map/all_gather | solution.py:177
  501.7 23.4 %all-to-all-start.3 = ((f32[4,1,98304]{2,1,0:T(1,128)}), f32[4,1,98304]{2,1,0:T(1,128)S(1)}, u32[]{:S(2)}, u32[]{:S(2)}) async-start(f32[4,1,98304]{2,1,0:T(1,128)} %broadcast_in_dim.31), calls=%async_computation.3 | async-start | bytes 3145728 | tf_op jit(solution)/shard_map/all_to_all | solution.py:42
  506.2 20.5 %copy-start.7 = (bf16[128,384]{1,0:T(8,128)(2,1)S(1)}, bf16[128,384]{1,0:T(8,128)(2,1)}, u32[]{:S(2)}) copy-start(bf16[128,384]{1,0:T(8,128)(2,1)} %get-tuple-element.112) | copy-start | bytes 294916
  506.2 44.5 %copy-start.6 = (f32[128,1536]{1,0:T(8,128)S(1)}, f32[128,1536]{1,0:T(8,128)}, u32[]{:S(2)}) copy-start(f32[128,1536]{1,0:T(8,128)} %copy-done.5) | copy-start | bytes 2359300
  528.6 27.6 %all-to-all-start.4 = ((f32[8,1,1]{2,1,0:T(1,128)}), f32[8,1,1]{2,1,0:T(1,128)S(1)}, u32[]{:S(2)}, u32[]{:S(2)}) async-start(f32[8,1,1]{2,1,0:T(1,128)} %broadcast_in_dim.32), calls=%async_computation.4 | async-start | bytes 8192 | tf_op jit(solution)/shard_map/all_to_all | solution.py:42
  533.9 142.7 %all-gather.6.cloned.1.call-start = ((), (), s32[]{:S(2)}) async-start(), calls=%async_computation.7 | async-start | bytes 3538944 | tf_op jit(solution)/shard_map/all_gather | solution.py:178
  572.0 1.3 copy-start.2
  574.3 37.7 %all-to-all-start.1 = ((bf16[128,8,384]{2,0,1:T(8,128)(2,1)}), bf16[128,8,384]{2,0,1:T(8,128)(2,1)S(1)}, u32[]{:S(2)}, u32[]{:S(2)}) async-start(bf16[128,8,384]{2,0,1:T(8,128)(2,1)} %bitcast.48), calls=%async_computation.1 | async-start | bytes 1572864 | tf_op jit(solution)/shard_map/all_to_all | solution.py:173
  612.0 25.6 %all-to-all-start.5 = ((bf16[128,8,384]{2,0,1:T(8,128)(2,1)}), bf16[128,8,384]{2,0,1:T(8,128)(2,1)S(1)}, u32[]{:S(2)}, u32[]{:S(2)}) async-start(bf16[128,8,384]{2,0,1:T(8,128)(2,1)} %bitcast.47), calls=%async_computation.5 | async-start | bytes 1572864 | tf_op jit(solution)/shard_map/all_to_all | solution.py:174
  676.6 5.3 copy-start.11
  684.7 2.0 copy-start.1
Sparse Core Ops, SparseCore 0:
  15.1 322.6 all-gather.3
  459.3 89.2 all-gather.7
  573.1 103.4 all-gather.5
where the time goes:
time: 698 us; the launch traced here: 693 us
  waiting for transfers between devices  463 us (66%)
  blocking collectives  102 us (15%)
  starting transfers between devices  38.4 us (6%)
  local copies, waits for them, and re-layouts  35.7 us (5%)
  matrix products  26.6 us (4%)
  between operations  15.4 us (2%)
  other arithmetic  11.5 us (2%)
    all_gather x1, waiting for transfers between devices, rows_first(): out = lax.all_gather(both, axis, axis=0, tiled=True)  306 us
    all_to_all x1, waiting for transfers between devices, sum_at_owner(): blocks = lax.all_to_all(split_up(shard, dim, count), axis, 0, 0, tiled=True)  40.8 us
    all_to_all x1, blocking collectives, sum_at_owner(): blocks = lax.all_to_all(split_up(shard, dim, count), axis, 0, 0, tiled=True)  40.6 us
    all_gather x1, waiting for transfers between devices, body(): lax.all_gather(pre_grad, 'rep', axis=0, tiled=True)  39 us
    all_to_all x1, waiting for transfers between devices, body(): lax.all_to_all(normed, 'rep', split_axis=1, concat_axis=0, tiled=True)  31.2 us
    all_gather x2, blocking collectives, front_pass(): whole_rows = lax.all_gather(inputs, 'tp', axis=1, tiled=True)  30.4 us
    all_to_all x1, waiting for transfers between devices, body(): lax.all_to_all(upstream, 'rep', split_axis=1, concat_axis=0, tiled=True)  22 us
    all_to_all x2, waiting for transfers between devices, sent_to_all(): return lax.all_to_all(copies, axis, split_axis=0, concat_axis=0, tiled=True)  18.9 us
  transfers between devices with their start and end apart: 10, of which 8 were waited for; matrix products, arithmetic and copies ran while one was open for 3% of the time, Pallas kernels for 0%

commit v1 on v0

v1 whole, which is shorter than its diff:
```python
import functools
import math

import jax
import jax.numpy as jnp
from jax import lax
from jax.experimental import pallas as pl
from jax.experimental.pallas import tpu as pltpu
from jax.sharding import PartitionSpec as P

MESH = pl.DeviceIdType.MESH
BF = jnp.bfloat16
F32 = jnp.float32
FEAT = 384
HID = 1536
EXT = 128
ROW = FEAT + EXT
WIDE = EXT + HID
CHUNKS = 2
HC = HID // CHUNKS
BLOCKS = 8
HALF = 64
QUARTER = 32
IMG_TOK = 128
D_ALL = 3072
TOKENS = 1024
GELU_C = math.sqrt(2.0 / math.pi)


def split_scalar(value):
    high = value.astype(BF).astype(F32)
    low = value - high
    lane = lax.broadcasted_iota(jnp.int32, (value.shape[0], EXT), 1)
    return jnp.where(lane < EXT // 2, high, low)


def join_scalar(columns):
    return columns[:, 0:1] + columns[:, EXT // 2 : EXT // 2 + 1]


def gelu_both(a):
    a2 = a * a
    th = jnp.tanh(GELU_C * a * (1.0 + 0.044715 * a2))
    half = 0.5 * (1.0 + th)
    grad = half + 0.5 * a * (1.0 - th * th) * (GELU_C * (1.0 + 3.0 * 0.044715 * a2))
    return a * half, grad


def wide_cols(c):
    return (0, EXT + HC) if c == 0 else (EXT + c * HC, HC)


def kernel(
    msgx, msgr, gain, up_hbm, down_hbm,
    gen_out, upg_out, dng_out,
    xt, rt, gen, gout, fk, dmine, dother,
    upw, dnw, xgs, hs, xgf, hf, dyb, dab, gd,
    sb1, rb1, po1, zs1, zr1, ts1, tr1,
    sb2, rb2, po2, zs2, zr2, ts2, tr2,
    sb3, rb3, po3, zs3, zr3,
    wsem, tsend, trecv, gsend, grecv,
    ag_s, ag_r, ry_s, ry_r, rz_s, rz_r, hy_s, hz_s, h_r, tp_s, tp_r,
):
    g, r, t = lax.axis_index("grp"), lax.axis_index("rep"), lax.axis_index("tp")
    y, zh = lax.div(r, 2), lax.rem(r, 2)
    half, quart = lax.rem(g, 2), lax.div(g, 2)
    g_pair = lax.rem(g + 2, 4)
    g_near = g + 1 - 2 * half
    late = (g >= 2).astype(jnp.int32)
    qrow = pl.multiple_of(quart * QUARTER, QUARTER)
    sends = []

    def dev(gg=None, rr=None, tt=None):
        return (g if gg is None else gg, r if rr is None else rr, t if tt is None else tt)

    def remote(src, dst, ssem, rsem, to, start=True, when=None):
        cp = pltpu.make_async_remote_copy(
            src_ref=src, dst_ref=dst, send_sem=ssem, recv_sem=rsem, device_id=to, device_id_type=MESH
        )
        if when is None:
            cp.start()
        else:
            pl.when(when)(cp.start)
        sends.append((cp, when))
        return cp

    def wait_recv(dst, rsem, when=None):
        cp = pltpu.make_async_remote_copy(
            src_ref=dst, dst_ref=dst, send_sem=rsem, recv_sem=rsem, device_id=dev(), device_id_type=MESH
        )
        if when is None:
            cp.wait_recv()
        else:
            pl.when(when)(cp.wait_recv)

    model = 1 + late
    loads = [
        pltpu.make_async_copy(up_hbm.at[0], upw.at[0], wsem.at[0]),
        pltpu.make_async_copy(down_hbm.at[0], dnw.at[0], wsem.at[1]),
        pltpu.make_async_copy(up_hbm.at[model], upw.at[1], wsem.at[2]),
        pltpu.make_async_copy(down_hbm.at[model], dnw.at[1], wsem.at[3]),
    ]
    for cp in loads:
        cp.start()

    barrier = pltpu.get_barrier_semaphore()
    for k in range(1, 8):
        pl.semaphore_signal(barrier, inc=1, device_id=dev(tt=lax.rem(t + k, 8)), device_id_type=MESH)
    for j in range(1, 4):
        pl.semaphore_signal(
            barrier, inc=1, device_id=dev(rr=2 * lax.rem(y + j, 4) + zh), device_id_type=MESH
        )
    pl.semaphore_signal(barrier, inc=1, device_id=dev(rr=2 * y + 1 - zh), device_id_type=MESH)
    pl.semaphore_signal(barrier, inc=1, device_id=dev(gg=g_pair), device_id_type=MESH)
    pl.semaphore_signal(barrier, inc=1, device_id=dev(gg=g_near), device_id_type=MESH)

    @pl.when(r != t)
    def _():
        pl.semaphore_signal(barrier, inc=1, device_id=dev(rr=t, tt=r), device_id_type=MESH)
        pl.semaphore_wait(barrier, 14)

    @pl.when(r == t)
    def _():
        pl.semaphore_wait(barrier, 13)

    off_diag = r != t
    flip = dev(rr=t, tt=r)
    remote(msgx, xt, tsend.at[0], trecv.at[0], flip, when=off_diag)
    remote(msgr, rt, tsend.at[1], trecv.at[1], flip, when=off_diag)

    @pl.when(jnp.logical_not(off_diag))
    def _():
        xt[...] = msgx[...]
        rt[...] = msgr[...]

    wait_recv(xt, trecv.at[0], off_diag)
    cond1 = 1.0 + xt[QUARTER : QUARTER + 1, :].astype(F32)

    def gather_tp(phase, block_of):
        for k in range(1, 8):
            remote(block_of(t), block_of(t), ag_s.at[phase, k], ag_r.at[phase, t], dev(tt=lax.rem(t + k, 8)))

    def wait_block(phase, block_of, b):
        wait_recv(block_of(b), ag_r.at[phase, b], b != t)

    def reduce_rep(phase, n, rows_of, block_of, product, sb, rb, po, zs, zr, finish):
        waited = set()
        zmine = pl.multiple_of(zh * n, n)
        zpeer = pl.multiple_of((1 - zh) * n, n)
        for c in range(CHUNKS):
            start, width = wide_cols(c)
            for j in (2, 1, 3, 0):
                yy = lax.rem(y + j, 4)
                if j not in waited:
                    waited.add(j)
                    wait_block(phase, block_of, 2 * yy)
                    wait_block(phase, block_of, 2 * yy + 1)
                rows = rows_of(yy)
                part = product(rows[:, :FEAT], c)
                if j:
                    if c == 0:
                        sb[j - 1, :, :EXT] = rows[:, FEAT:]
                        sb[j - 1, :, EXT : EXT + HC] = part.astype(BF)
                    else:
                        sb[j - 1, :, start : start + width] = part.astype(BF)
                    cols = (j - 1, slice(None), pl.ds(start, width))
                    remote(
                        sb.at[cols], rb.at[cols], ry_s.at[phase, c, j], ry_r.at[phase, c, j],
                        dev(rr=2 * yy + zh),
                    )
                else:
                    if c == 0:
                        po[:, :EXT] = rows[:, FEAT:].astype(F32)
                        po[:, EXT : EXT + HC] = part
                    else:
                        po[:, start : start + width] = part
        peer = dev(rr=2 * y + 1 - zh)
        for c in range(CHUNKS):
            start, width = wide_cols(c)
            for j in (1, 3, 2):
                wait_recv(rb.at[j - 1, :, pl.ds(start, width)], ry_r.at[phase, c, j])

            def summed(row, lo, wid):
                total = po[pl.ds(row, n), lo : lo + wid]
                for j in range(3):
                    total += rb[j, pl.ds(row, n), lo : lo + wid].astype(F32)
                return total

            if c == 0:
                zs[:, :EXT] = split_scalar(join_scalar(summed(zpeer, 0, EXT))).astype(BF)
            lo = EXT + c * HC
            zs[:, lo : lo + HC] = summed(zpeer, lo, HC).astype(BF)
            remote(
                zs.at[:, pl.ds(start, width)], zr.at[:, pl.ds(start, width)],
                rz_s.at[phase, c], rz_r.at[phase, c], peer,
            )
        row_scalar = None
        for c in range(CHUNKS):
            start, width = wide_cols(c)
            wait_recv(zr.at[:, pl.ds(start, width)], rz_r.at[phase, c])

            def summed(lo, wid):
                total = po[pl.ds(zmine, n), lo : lo + wid] + zr[:, lo : lo + wid].astype(F32)
                for j in range(3):
                    total += rb[j, pl.ds(zmine, n), lo : lo + wid].astype(F32)
                return total

            if c == 0:
                row_scalar = join_scalar(summed(0, EXT))
            finish(c, summed(EXT + c * HC, HC), row_scalar)

    def gather_rep_own(phase, c, piece):
        remote(piece(r), piece(r), hz_s.at[phase, c], h_r.at[phase, c, r], dev(rr=2 * y + 1 - zh))
        for j in (2, 1, 3):
            yy = lax.rem(y + j, 4)
            remote(piece(r), piece(r), hy_s.at[phase, c, 0, j], h_r.at[phase, c, r], dev(rr=2 * yy + zh))

    def gather_rep_pass(phase, c, piece):
        b = 2 * y + 1 - zh
        wait_recv(piece(b), h_r.at[phase, c, b])
        for j in (2, 1, 3):
            yy = lax.rem(y + j, 4)
            remote(piece(b), piece(b), hy_s.at[phase, c, 1, j], h_r.at[phase, c, b], dev(rr=2 * yy + zh))

    def wait_rep(phase, c, piece, b):
        wait_recv(piece(b), h_r.at[phase, c, b])

    def forward(phase, n, x_rows, gain_row, xg, xg_rows, h, h_rows, up, down, grad, sb, rb, po, zs, zr, ts, tr):
        xg[t, xg_rows, :FEAT] = (x_rows * (gain_row * cond1)).astype(BF)
        xg[t, xg_rows, FEAT:] = split_scalar(jnp.sum(x_rows * x_rows, axis=1, keepdims=True)).astype(BF)
        block_of = lambda b: xg.at[b, xg_rows, :]
        gather_tp(phase, block_of)
        rows_of = lambda yy: xg[pl.ds(2 * yy, 2), xg_rows, :].reshape(2 * n, ROW)
        loads[2 * phase].wait()

        def product(rows, c):
            return jnp.dot(rows, up[:, c * HC : (c + 1) * HC], preferred_element_type=F32)

        def piece_of(c):
            return lambda b: h.at[b, h_rows, pl.ds(c * HC, HC)]

        def finish(c, a, square_sum):
            factor = lax.rsqrt(square_sum * (1.0 / D_ALL) + 1e-6)
            hidden, slope = gelu_both(a * factor)
            h[r, h_rows, c * HC : (c + 1) * HC] = hidden.astype(BF)
            grad[h_rows, c * HC : (c + 1) * HC] = (slope * factor).astype(BF)
            gather_rep_own(phase, c, piece_of(c))

        reduce_rep(phase, n, rows_of, block_of, product, sb, rb, po, zs, zr, finish)
        for c in range(CHUNKS):
            gather_rep_pass(phase, c, piece_of(c))
        loads[2 * phase + 1].wait()
        for j in (0, 1, 3, 2):
            yy = lax.rem(y + j, 4)
            if j:
                for c in range(CHUNKS):
                    wait_rep(phase, c, piece_of(c), 2 * yy + zh)
                    wait_rep(phase, c, piece_of(c), 2 * yy + 1 - zh)
            both = h[pl.ds(2 * yy, 2), h_rows, :].reshape(2 * n, HID)
            part = jnp.dot(both, down[...], preferred_element_type=F32)
            ts[pl.ds(2 * yy, 2)] = part.astype(BF).reshape(2, n, FEAT)
            for k in range(2):
                b = 2 * yy + k
                remote(ts.at[b], tr.at[t], tp_s.at[phase, b], tp_r.at[phase, t], dev(tt=b), when=b != t)
        total = ts[t].astype(F32)
        for k in range(1, 8):
            b = lax.rem(t + k, 8)
            wait_recv(tr.at[b], tp_r.at[phase, b])
            total += tr[b].astype(F32)
        return total

    x0 = xt[:QUARTER, :].astype(F32)
    q_rows = pl.ds(qrow, QUARTER)
    out = forward(
        0, QUARTER, x0, gain[0:1, :], xgs, q_rows, hs, q_rows, upw.at[0], dnw.at[0], gd.at[0],
        sb1, rb1, po1, zs1, zr1, ts1, tr1,
    )
    own = pl.ds(pl.multiple_of(half * HALF + quart * QUARTER, QUARTER), QUARTER)
    pair = pl.ds(pl.multiple_of(half * HALF + (1 - quart) * QUARTER, QUARTER), QUARTER)
    mine = pl.ds(pl.multiple_of(half * HALF, HALF), HALF)
    other = pl.ds(pl.multiple_of((1 - half) * HALF, HALF), HALF)
    gen[own, :] = (x0 + out).astype(BF)
    remote(gen.at[own, :], gen.at[own, :], gsend.at[0], grecv.at[0], dev(gg=g_pair))
    is_late = g >= 2
    is_early = g < 2
    for i, ref in enumerate((xgs.at[:, q_rows, :], hs.at[:, q_rows, :], gd.at[0, q_rows, :])):
        remote(ref, ref, gsend.at[1 + i], grecv.at[1 + i], dev(gg=g_pair), when=is_late)
    wait_recv(gen.at[pair, :], grecv.at[0])
    remote(gen.at[mine, :], gen.at[mine, :], gsend.at[4], grecv.at[4], dev(gg=g_near))

    wait_recv(rt, trecv.at[1], off_diag)
    t_row = xt[QUARTER + 8 : QUARTER + 9, :].astype(F32)
    t_value = t_row[:, 0:1] * 256.0 + t_row[:, EXT : EXT + 1]
    sigma = 0.1 + 0.8 * t_value / 999.0
    gen_f = gen[mine, :].astype(F32)
    x_t = ((1.0 - sigma) * gen_f + sigma * rt[...].astype(F32)).astype(BF).astype(F32)
    all_rows = pl.ds(0, HALF)
    out = forward(
        1, HALF, x_t, gain[pl.ds(model, 1), :], xgf.at[half], all_rows, hf.at[half], all_rows,
        upw.at[1], dnw.at[1], gd.at[1], sb2, rb2, po2, zs2, zr2, ts2, tr2,
    )
    pred = (x_t + out).astype(BF)
    is_2, is_3 = g == 2, g == 3
    for i, ref in enumerate((xgf.at[0], hf.at[0])):
        remote(ref, ref, gsend.at[5 + i], grecv.at[5 + i], dev(gg=g_near), when=is_2)

    wait_recv(gen.at[other, :], grecv.at[4])
    remote(gen, gout, tsend.at[2], trecv.at[2], flip, when=off_diag)

    scale = 1.0 / math.sqrt(TOKENS)
    fk[...] = pred

    def to_pair():
        pltpu.make_async_remote_copy(
            src_ref=fk, dst_ref=dother.at[0], send_sem=gsend.at[7], recv_sem=grecv.at[7],
            device_id=dev(gg=g_pair), device_id_type=MESH,
        ).start()

    pl.when(is_late)(to_pair)
    dy = dyb.at[half]

    @pl.when(is_late)
    def _():
        dy[t, :, :FEAT] = ((fk[...].astype(F32) - gen_f) * scale).astype(BF)
        dy[t, :, FEAT:] = jnp.zeros((HALF, EXT), BF)

    @pl.when(is_early)
    def _():
        real = fk[...].astype(F32)
        distance = jnp.sum(jnp.sum(jnp.abs(gen_f - real), axis=1, keepdims=True), axis=0, keepdims=True)
        dmine[0] = jnp.broadcast_to(distance, (8, EXT))
        cp = pltpu.make_async_remote_copy(
            src_ref=dmine.at[0], dst_ref=dmine.at[1], send_sem=gsend.at[8], recv_sem=grecv.at[8],
            device_id=dev(gg=g_near), device_id_type=MESH,
        )
        cp.start()
        wait_recv(dother.at[0], grecv.at[7])
        fake = dother[0].astype(F32)
        dy[t, :, :FEAT] = ((fake - real) * scale).astype(BF)
        cp.wait()
        both = jnp.broadcast_to(dmine[0, 0:1, 0:1] + dmine[1, 0:1, 0:1], (HALF, 1))
        dy[t, :, FEAT:] = split_scalar(both).astype(BF)

    dy_block = lambda b: dy.at[b]
    gather_tp(2, dy_block)
    da = dab.at[half]
    back = dnw.at[late]
    slope = gd.at[late]

    def product(rows, c):
        return lax.dot_general(
            rows, back[c * HC : (c + 1) * HC, :], (((1,), (1,)), ((), ())), preferred_element_type=F32
        )

    def da_piece(c):
        start, width = wide_cols(c)
        return lambda b: da.at[b, :, pl.ds(start, width)]

    wait_recv(gd.at[0, pl.ds(QUARTER, QUARTER), :], grecv.at[3], is_early)

    def finish(c, dh, distance):
        norm = distance * (1.0 / (IMG_TOK * D_ALL)) + 1e-5
        row_scale = jnp.where(is_late, 1.0, 1.0 / norm)
        lo = EXT + c * HC
        if c == 0:
            da[r, :, :EXT] = split_scalar(row_scale).astype(BF)
        da[r, :, lo : lo + HC] = (dh * row_scale * slope[:, c * HC : (c + 1) * HC].astype(F32)).astype(BF)
        gather_rep_own(2, c, da_piece(c))

    reduce_rep(
        2, HALF, lambda yy: dy[pl.ds(2 * yy, 2)].reshape(2 * HALF, ROW), dy_block, product,
        sb3, rb3, po3, zs3, zr3, finish,
    )
    remote(dyb.at[0], dyb.at[0], gsend.at[9], grecv.at[9], dev(gg=g_near), when=is_2)
    for c in range(CHUNKS):
        gather_rep_pass(2, c, da_piece(c))
    relay = lambda b: remote(dab.at[0, b], dab.at[0, b], gsend.at[10 + b], grecv.at[10 + b], dev(gg=g_near), when=is_2)
    relay(r)
    relay(2 * y + 1 - zh)
    for j in (1, 3, 2):
        yy = lax.rem(y + j, 4)
        for b in (2 * yy + zh, 2 * yy + 1 - zh):
            for c in range(CHUNKS):
                wait_rep(2, c, da_piece(c), b)
            relay(b)

    for i, ref in enumerate((xgs.at[:, pl.ds(QUARTER, QUARTER), :], hs.at[:, pl.ds(QUARTER, QUARTER), :])):
        wait_recv(ref, grecv.at[1 + i], is_early)
    for i, ref in enumerate((xgf.at[0], hf.at[0])):
        wait_recv(ref, grecv.at[5 + i], is_3)
    wait_recv(dyb.at[0], grecv.at[9], is_3)
    for b in range(BLOCKS):
        wait_recv(dab.at[0, b], grecv.at[10 + b], is_3)

    tn = (((0,), (0,)), ((), ()))
    step = 256

    def weight_grads(tokens, u_of, da_of, h_of, dy_of):
        def up_tile(i, _):
            cols = pl.ds(pl.multiple_of(i * step, step), step)
            wide = pl.ds(pl.multiple_of(EXT + i * step, EXT), step)
            upg_out[0, :, cols] = lax.dot_general(u_of(), da_of(wide), tn, preferred_element_type=F32)
            return 0

        lax.fori_loop(0, HID // step, up_tile, 0)
        row_scale = join_scalar(da_of(slice(0, EXT)).astype(F32))
        upstream = (dy_of().astype(F32) * row_scale).astype(BF)

        def down_tile(i, _):
            cols = pl.ds(pl.multiple_of(i * step, step), step)
            dng_out[0, cols, :] = lax.dot_general(h_of(cols), upstream, tn, preferred_element_type=F32)
            return 0

        lax.fori_loop(0, HID // step, down_tile, 0)

    @pl.when(is_early)
    def _():
        n = BLOCKS * HALF
        weight_grads(
            n,
            lambda: xgs[:, :, :FEAT].reshape(n, FEAT),
            lambda cols: da[:, :, cols].reshape(n, -1),
            lambda cols: hs[:, :, cols].reshape(n, -1),
            lambda: dy[:, :, :FEAT].reshape(n, FEAT),
        )

    @pl.when(is_2)
    def _():
        upg_out[...] = jnp.zeros_like(upg_out)
        dng_out[...] = jnp.zeros_like(dng_out)

    @pl.when(is_3)
    def _():
        n = 2 * BLOCKS * HALF
        weight_grads(
            n,
            lambda: xgf[:, :, :, :FEAT].reshape(n, FEAT),
            lambda cols: dab[:, :, :, cols].reshape(n, -1),
            lambda cols: hf[:, :, :, cols].reshape(n, -1),
            lambda: dyb[:, :, :, :FEAT].reshape(n, FEAT),
        )

    wait_recv(gout, trecv.at[2], off_diag)

    @pl.when(off_diag)
    def _():
        gen_out[...] = gout[...]

    @pl.when(jnp.logical_not(off_diag))
    def _():
        gen_out[...] = gen[...]

    for cp, when in sends:
        if when is None:
            cp.wait_send()
        else:
            pl.when(when)(cp.wait_send)

    @pl.when(is_late)
    def _():
        pltpu.make_async_remote_copy(
            src_ref=fk, dst_ref=dother.at[0], send_sem=gsend.at[7], recv_sem=grecv.at[7],
            device_id=dev(gg=g_pair), device_id_type=MESH,
        ).wait_send()


def rep_buffers(n):
    return [
        pltpu.VMEM((3, 2 * n, WIDE), BF),
        pltpu.VMEM((3, 2 * n, WIDE), BF),
        pltpu.VMEM((2 * n, WIDE), F32),
        pltpu.VMEM((n, WIDE), BF),
        pltpu.VMEM((n, WIDE), BF),
    ]


def body(noise_in, noise_renoise, text_cond, t_index, gains, up_weights, down_weights):
    g, r, t = lax.axis_index("grp"), lax.axis_index("rep"), lax.axis_index("tp")
    half, quart = g % 2, g // 2
    x_part = lax.dynamic_slice_in_dim(noise_in, half * HALF + quart * QUARTER, QUARTER, 0)
    r_part = lax.dynamic_slice_in_dim(noise_renoise, half * HALF, HALF, 0)
    cond = lax.dynamic_slice_in_dim(text_cond, t * FEAT, FEAT, 1)
    t_all = t_index.astype(F32)
    t_high = jnp.floor(t_all * (1.0 / 256.0))
    t_low = t_all - 256.0 * t_high
    lane = lax.broadcasted_iota(jnp.int32, (8, FEAT), 1)
    t_rows = jnp.where(lane < EXT, t_high, t_low).astype(BF)
    msgx = jnp.concatenate([x_part, jnp.broadcast_to(cond, (8, FEAT)), t_rows], axis=0)
    gain = jnp.pad(lax.dynamic_slice_in_dim(gains, r * FEAT, FEAT, 1), ((0, 5), (0, 0)))
    vmem = pl.BlockSpec(memory_space=pltpu.VMEM)
    hbm = pl.BlockSpec(memory_space=pl.ANY)
    dma = pltpu.SemaphoreType.DMA
    tp_buffers = lambda n: [pltpu.VMEM((BLOCKS, n, FEAT), BF)] * 2
    out = pl.pallas_call(
        kernel,
        name="step",
        out_shape=(
            jax.ShapeDtypeStruct((IMG_TOK, FEAT), BF),
            jax.ShapeDtypeStruct((1, FEAT, HID), F32),
            jax.ShapeDtypeStruct((1, HID, FEAT), F32),
        ),
        in_specs=[vmem, vmem, vmem, hbm, hbm],
        out_specs=(vmem, vmem, vmem),
        scratch_shapes=[
            pltpu.VMEM((QUARTER + 16, FEAT), BF),
            pltpu.VMEM((HALF, FEAT), BF),
            pltpu.VMEM((IMG_TOK, FEAT), BF),
            pltpu.VMEM((IMG_TOK, FEAT), BF),
            pltpu.VMEM((HALF, FEAT), BF),
            pltpu.VMEM((2, 8, EXT), F32),
            pltpu.VMEM((1, HALF, FEAT), BF),
            pltpu.VMEM((2, FEAT, HID), BF),
            pltpu.VMEM((2, HID, FEAT), BF),
            pltpu.VMEM((BLOCKS, HALF, ROW), BF),
            pltpu.VMEM((BLOCKS, HALF, HID), BF),
            pltpu.VMEM((2, BLOCKS, HALF, ROW), BF),
            pltpu.VMEM((2, BLOCKS, HALF, HID), BF),
            pltpu.VMEM((2, BLOCKS, HALF, ROW), BF),
            pltpu.VMEM((2, BLOCKS, HALF, WIDE), BF),
            pltpu.VMEM((2, HALF, HID), BF),
            *rep_buffers(QUARTER),
            *tp_buffers(QUARTER),
            *rep_buffers(HALF),
            *tp_buffers(HALF),
            *rep_buffers(HALF),
            dma((4,)),
            dma((3,)),
            dma((3,)),
            dma((18,)),
            dma((18,)),
            dma((3, 8)),
            dma((3, 8)),
            dma((3, CHUNKS, 4)),
            dma((3, CHUNKS, 4)),
            dma((3, CHUNKS)),
            dma((3, CHUNKS)),
            dma((3, CHUNKS, 2, 4)),
            dma((3, CHUNKS)),
            dma((3, CHUNKS, 8)),
            dma((2, 8)),
            dma((2, 8)),
        ],
        compiler_params=pltpu.CompilerParams(
            collective_id=0, has_side_effects=True, vmem_limit_bytes=60 * 2**20
        ),
    )(msgx, r_part, gain, up_weights, down_weights)
    return out


def solution(mesh):
    in_specs = (
        P("rep", "tp"),
        P("rep", "tp"),
        P("rep", None),
        P("rep"),
        P(),
        P(None, "rep", "tp"),
        P(None, "tp", "rep"),
    )
    out_specs = (P("rep", "tp"), P("grp", "rep", "tp"), P("grp", "tp", "rep"))
    return jax.shard_map(body, mesh=mesh, in_specs=in_specs, out_specs=out_specs, check_vma=False)
```

time: 698 us -> 253 us (0.36)
  the two profiles are of different devices: /device:TPU:102 before, /device:TPU:1 now
where the time goes in v1:
time: 253 us
  Pallas kernels  241 us (95%)
  local copies, waits for them, and re-layouts  9.72 us (4%)
    pallas_call x1, Pallas kernels, body(): pl.pallas_call(kernel, name='step', out_shape=(jax.ShapeDtypeStruct((IMG_...  241 us
    unnamed x7, local copies, waits for them, and re-layouts  6.33 us

profile of v1, /device:TPU:1, one launch (start us, length us, event | category | flops | bytes accessed | tf_op | source)
XLA Modules:
  0.0 252.9 jit_solution(12908527392093774630)
XLA Ops:
  0.6 0.0 copy-start
  1.4 0.7 dynamic-slice_reduce_fusion
  2.1 0.7 constant_dynamic-slice_fusion
  2.8 0.6 pad.4.gain
  3.4 0.7 constant_dynamic-slice_fusion.2
  4.1 0.6 pad_maximum_fusion.msgx
  4.8 0.0 copy-done
  4.8 0.6 constant_dynamic-slice_fusion.1.msgr
  5.4 241.2 %step.1 = (bf16[128,384]{1,0:T(8,128)(2,1)}, f32[1,384,1536]{2,1,0:T(8,128)}, f32[1,1536,384]{2,1,0:T(8,128)}) custom-call(bf16[48,384]{1,0:T(8,128)(2,1)} %pad_maximum_fusion.msgx, bf16[64,384]{1,0:T(8,128)(2,1)} %constant_dynamic-slice_fusion.1.msgr, f32[8,384]{1,0:T(8,128)} %pad.4.gain, bf16[3,384,1536]{2,1,0:T(8,128)(2,1)} %up_hbm.1, ...), custom_call_target="tpu_custom_call" | custom-call | tf_op jit(solution)/shard_map/step/pallas_call | solution.py:494
  246.6 1.5 copy.14
  248.1 0.0 copy-start.1
  248.1 3.4 %copy.15 = f32[1,384,1536]{2,1,0:T(8,128)} copy(f32[1,384,1536]{2,1,0:T(8,128)} %get-tuple-element.7) | data formatting | bytes 4718592
  251.5 0.0 copy-done.1
  251.5 1.4 copy.16
  (3 shorter events, 0.0 us)
Async XLA Ops:
  0.6 4.1 %copy-start = (bf16[128,384]{1,0:T(8,128)(2,1)S(1)}, bf16[128,384]{1,0:T(8,128)(2,1)}, u32[]{:S(2)}) copy-start(bf16[128,384]{1,0:T(8,128)(2,1)} %param.8) | copy-start | bytes 294916
  248.1 3.4 %copy-start.1 = (f32[1,1536,384]{2,1,0:T(8,128)S(1)}, f32[1,1536,384]{2,1,0:T(8,128)}, u32[]{:S(2)}) copy-start(f32[1,1536,384]{2,1,0:T(8,128)} %get-tuple-element.8) | copy-start | bytes 7077892

commit v2 on v1

v2 whole, which is shorter than its diff:
```python
import functools
import math

import jax
import jax.numpy as jnp
from jax import lax
from jax.experimental import pallas as pl
from jax.experimental.pallas import tpu as pltpu
from jax.sharding import PartitionSpec as P

MESH = pl.DeviceIdType.MESH
BF = jnp.bfloat16
F32 = jnp.float32
FEAT = 384
HID = 1536
EXT = 128
ROW = FEAT + EXT
WIDE = EXT + HID
CHUNKS = 4
HC = HID // CHUNKS
BLOCKS = 8
HALF = 64
QUARTER = 32
IMG_TOK = 128
D_ALL = 3072
TOKENS = 1024
GELU_C = math.sqrt(2.0 / math.pi)


def split_scalar(value):
    high = value.astype(BF).astype(F32)
    low = value - high
    lane = lax.broadcasted_iota(jnp.int32, (value.shape[0], EXT), 1)
    return jnp.where(lane < EXT // 2, high, low)


def join_scalar(columns):
    return columns[:, 0:1] + columns[:, EXT // 2 : EXT // 2 + 1]


def gelu_both(a):
    a2 = a * a
    th = jnp.tanh(GELU_C * a * (1.0 + 0.044715 * a2))
    half = 0.5 * (1.0 + th)
    grad = half + 0.5 * a * (1.0 - th * th) * (GELU_C * (1.0 + 3.0 * 0.044715 * a2))
    return a * half, grad


def wide_cols(c):
    return (0, EXT + HC) if c == 0 else (EXT + c * HC, HC)


def kernel(
    noise, renoise, cond_in, t_in, gains, up_hbm, down_hbm,
    gen_out, upg_out, dng_out,
    msgc, xt, ct, rt, gen, gout, fk, fother, dmine,
    upw, dnw, xgs, hs, xgf, hf, dyb, dab, gd,
    sb1, rb1, po1, zs1, zr1, acc1, ta1, tb1, tc1, td1,
    sb2, rb2, po2, zs2, zr2, acc2, ta2, tb2, tc2, td2,
    sb3, rb3, po3, zs3, zr3,
    wsem, tsend, trecv, gsend, grecv,
    ag_s, ag_r, ry_s, ry_r, rz_s, rz_r, hy_s, h_r, tp_s, tp_r, xs_s, xs_r,
):
    g, r, t = lax.axis_index("grp"), lax.axis_index("rep"), lax.axis_index("tp")
    y, zh = lax.div(r, 2), lax.rem(r, 2)
    zl, core = lax.div(t, 2), lax.rem(t, 2)
    is_late, is_early = g >= 2, g < 2
    is_2, is_3 = g == 2, g == 3
    late = is_late.astype(jnp.int32)
    quart = late
    low = lax.rem(g, 2)
    half = low + late - 2 * low * late
    g_pair = 3 - g
    g_near = g + 1 - 2 * low
    qrow = pl.multiple_of(quart * QUARTER, QUARTER)
    sends = []

    def dev(gg=None, rr=None, tt=None):
        return (g if gg is None else gg, r if rr is None else rr, t if tt is None else tt)

    def remote(src, dst, ssem, rsem, to, when=None):
        cp = pltpu.make_async_remote_copy(
            src_ref=src, dst_ref=dst, send_sem=ssem, recv_sem=rsem, device_id=to, device_id_type=MESH
        )
        if when is None:
            cp.start()
        else:
            pl.when(when)(cp.start)
        sends.append((cp, when))
        return cp

    def wait_recv(dst, rsem, when=None):
        cp = pltpu.make_async_remote_copy(
            src_ref=dst, dst_ref=dst, send_sem=rsem, recv_sem=rsem, device_id=dev(), device_id_type=MESH
        )
        if when is None:
            cp.wait_recv()
        else:
            pl.when(when)(cp.wait_recv)

    model = 1 + late
    loads = [
        pltpu.make_async_copy(up_hbm.at[0], upw.at[0], wsem.at[0]),
        pltpu.make_async_copy(down_hbm.at[0], dnw.at[0], wsem.at[1]),
        pltpu.make_async_copy(up_hbm.at[model], upw.at[1], wsem.at[2]),
        pltpu.make_async_copy(down_hbm.at[model], dnw.at[1], wsem.at[3]),
    ]
    for cp in loads:
        cp.start()

    barrier = pltpu.get_barrier_semaphore()
    sibling = dev(tt=2 * zl + 1 - core)
    flip = dev(rr=t, tt=r)
    off_diag = r != t
    row_peer = lambda yy: dev(rr=2 * yy + zh)
    z_peer = dev(rr=2 * y + 1 - zh)
    peers = [sibling, z_peer, dev(gg=g_pair), dev(gg=g_near)]
    peers += [dev(tt=2 * lax.rem(zl + d, 4) + core) for d in range(1, 4)]
    peers += [row_peer(lax.rem(y + j, 4)) for j in range(1, 4)]
    for peer in peers:
        pl.semaphore_signal(barrier, inc=1, device_id=peer, device_id_type=MESH)

    cond_row = cond_in[0:1, pl.ds(pl.multiple_of(t * FEAT, EXT), FEAT)].astype(F32)
    t_all = jnp.full((16, FEAT), t_in[0], jnp.int32)
    row = lax.broadcasted_iota(jnp.int32, (16, FEAT), 0)
    lane = lax.broadcasted_iota(jnp.int32, (16, FEAT), 1)
    t_part = jnp.where(lane < EXT, t_all >> 8, t_all & 255).astype(F32)
    msgc[...] = jnp.where(row < 8, jnp.broadcast_to(cond_row, (16, FEAT)), t_part).astype(BF)

    @pl.when(off_diag)
    def _():
        pl.semaphore_signal(barrier, inc=1, device_id=flip, device_id_type=MESH)
        pl.semaphore_wait(barrier, len(peers) + 1)

    @pl.when(jnp.logical_not(off_diag))
    def _():
        pl.semaphore_wait(barrier, len(peers))

    own = pl.ds(pl.multiple_of(half * HALF + quart * QUARTER, QUARTER), QUARTER)
    pair = pl.ds(pl.multiple_of(half * HALF + (1 - quart) * QUARTER, QUARTER), QUARTER)
    mine = pl.ds(pl.multiple_of(half * HALF, HALF), HALF)
    other = pl.ds(pl.multiple_of((1 - half) * HALF, HALF), HALF)
    remote(noise.at[own, :], xt, tsend.at[0], trecv.at[0], flip, when=off_diag)
    remote(msgc, ct, tsend.at[1], trecv.at[1], flip, when=off_diag)
    remote(renoise.at[mine, :], rt, tsend.at[2], trecv.at[2], flip, when=off_diag)

    @pl.when(jnp.logical_not(off_diag))
    def _():
        xt[...] = noise[own, :]
        ct[...] = msgc[...]
        rt[...] = renoise[mine, :]

    wait_recv(xt, trecv.at[0], off_diag)
    wait_recv(ct, trecv.at[1], off_diag)
    cond1 = 1.0 + ct[0:1, :].astype(F32)

    def gather_tp(phase, block_of):
        remote(block_of(t), block_of(t), ag_s.at[phase, 0], ag_r.at[phase, t], sibling)
        for d in (2, 1, 3):
            to = dev(tt=2 * lax.rem(zl + d, 4) + core)
            remote(block_of(t), block_of(t), ag_s.at[phase, d], ag_r.at[phase, t], to)

    def wait_chip(phase, block_of, d):
        yy = lax.rem(zl + d, 4)
        if d:
            b = 2 * yy + core
            wait_recv(block_of(b), ag_r.at[phase, b])
            remote(block_of(b), block_of(b), ag_s.at[phase, 3 + d], ag_r.at[phase, b], sibling)
        b = 2 * yy + 1 - core
        wait_recv(block_of(b), ag_r.at[phase, b])

    def reduce_rep(phase, n, rows_of, block_of, product, bufs, finish, gathered):
        sb, rb, po, zs, zr = bufs
        for c in range(CHUNKS):
            start, width = wide_cols(c)
            lo = EXT + c * HC
            for d in (0, 1, 3, 2):
                yy = lax.rem(zl + d, 4)
                if c == 0:
                    wait_chip(phase, block_of, d)
                rows = rows_of(yy)
                part = product(rows[:, :FEAT], c)

                @pl.when(yy == y)
                def _():
                    if c == 0:
                        po[:, :EXT] = rows[:, FEAT:].astype(F32)
                    po[:, lo : lo + HC] = part

                @pl.when(yy != y)
                def _():
                    if c == 0:
                        sb[yy, :, :EXT] = rows[:, FEAT:]
                    sb[yy, :, lo : lo + HC] = part.astype(BF)

                cols = pl.ds(start, width)
                remote(
                    sb.at[yy, :, cols], rb.at[y, :, cols], ry_s.at[phase, c, d], ry_r.at[phase, c, y],
                    row_peer(yy), when=yy != y,
                )
            if c == 0:
                gathered()

        def to_z(c):
            start, width = wide_cols(c)
            others = [lax.rem(y + j, 4) for j in (1, 3, 2)]
            for yy in others:
                wait_recv(rb.at[yy, :, pl.ds(start, width)], ry_r.at[phase, c, yy])

            def add_up(lo, wid):
                total = po[:, lo : lo + wid]
                for yy in others:
                    total += rb[yy, :, lo : lo + wid].astype(F32)
                po[:, lo : lo + wid] = total
                return total

            if c == 0:
                zs[:, :EXT] = split_scalar(join_scalar(add_up(0, EXT))).astype(BF)
            lo = EXT + c * HC
            zs[:, lo : lo + HC] = add_up(lo, HC).astype(BF)
            cols = pl.ds(start, width)
            remote(zs.at[:, cols], zr.at[:, cols], rz_s.at[phase, c], rz_r.at[phase, c], z_peer)

        state = {}

        def from_z(c):
            start, width = wide_cols(c)
            wait_recv(zr.at[:, pl.ds(start, width)], rz_r.at[phase, c])
            if c == 0:
                state["scalar"] = join_scalar(po[:, :EXT] + zr[:, :EXT].astype(F32))
            lo = EXT + c * HC
            finish(c, po[:, lo : lo + HC] + zr[:, lo : lo + HC].astype(F32), state["scalar"])

        ahead = CHUNKS - 1 if n == HALF else CHUNKS
        for c in range(CHUNKS):
            if c == ahead:
                from_z(0)
            to_z(c)
        for c in range(1 if ahead < CHUNKS else 0, CHUNKS):
            from_z(c)

    def forward(phase, n, x_rows, gain_row, xg, xg_rows, h, h_rows, bufs, gathered, chunk_here):
        acc, ta, tb, tc, td = bufs[5:]
        up, down, grad = upw.at[phase], dnw.at[phase], gd.at[phase]
        xg[t, xg_rows, :FEAT] = (x_rows * (gain_row * cond1)).astype(BF)
        xg[t, xg_rows, FEAT:] = split_scalar(jnp.sum(x_rows * x_rows, axis=1, keepdims=True)).astype(BF)
        block_of = lambda b: xg.at[b, xg_rows, :]
        gather_tp(phase, block_of)
        rows_of = lambda yy: xg[pl.ds(2 * yy, 2), xg_rows, :].reshape(2 * n, ROW)
        loads[2 * phase].wait()

        def product(rows, c):
            return jnp.dot(rows, up[:, c * HC : (c + 1) * HC], preferred_element_type=F32)

        piece = lambda yy, c: h.at[pl.ds(2 * yy, 2), h_rows, pl.ds(c * HC, HC)]

        def finish(c, a, square_sum):
            factor = lax.rsqrt(square_sum * (1.0 / D_ALL) + 1e-6)
            hidden, slope = gelu_both(a * factor)
            cols = slice(c * HC, (c + 1) * HC)
            h[pl.ds(2 * y, 2), h_rows, cols] = hidden.astype(BF).reshape(2, n, HC)
            for j in (2, 1, 3):
                remote(
                    piece(y, c), piece(y, c), hy_s.at[phase, c, j], h_r.at[phase, c, y],
                    row_peer(lax.rem(y + j, 4)),
                )
            grad[:, h_rows, cols] = (slope * factor).astype(BF).reshape(2, n, HC)

        reduce_rep(phase, n, rows_of, block_of, product, bufs[:5], finish, gathered)
        loads[2 * phase + 1].wait()
        for c in range(CHUNKS):
            cols = slice(c * HC, (c + 1) * HC)
            for j in (0, 1, 3, 2):
                yy = lax.rem(y + j, 4)
                if j:
                    wait_recv(piece(yy, c), h_r.at[phase, c, yy])
                both = h[pl.ds(2 * yy, 2), h_rows, cols].reshape(2 * n, HC)
                part = jnp.dot(both, down[cols, :], preferred_element_type=F32).reshape(2, n, FEAT)
                if c:
                    acc[pl.ds(2 * yy, 2)] += part
                else:
                    acc[pl.ds(2 * yy, 2)] = part
            chunk_here(c)
        for d in (2, 1, 3, 0):
            yy = lax.rem(zl + d, 4)
            ta[d] = acc[2 * yy + 1 - core].astype(BF)
            remote(ta.at[d], tb.at[d], tp_s.at[phase, d], tp_r.at[phase, d], sibling)
        total = None
        for d in (2, 1, 3, 0):
            yy = lax.rem(zl + d, 4)
            wait_recv(tb.at[d], tp_r.at[phase, d])
            both = acc[2 * yy + core] + tb[d].astype(F32)
            if d:
                tc[d - 1] = both.astype(BF)
                remote(
                    tc.at[d - 1], td.at[d - 1], tp_s.at[phase, 3 + d], tp_r.at[phase, 3 + d],
                    dev(tt=2 * yy + core),
                )
            else:
                total = both
        for d in (1, 3, 2):
            wait_recv(td.at[d - 1], tp_r.at[phase, 3 + d])
            total += td[d - 1].astype(F32)
        return total

    gain = gains[:, pl.ds(pl.multiple_of(r * FEAT, EXT), FEAT)]
    x0 = xt[...].astype(F32)
    q_rows = pl.ds(qrow, QUARTER)
    out = forward(
        0, QUARTER, x0, gain[0:1, :], xgs, q_rows, hs, q_rows,
        (sb1, rb1, po1, zs1, zr1, acc1, ta1, tb1, tc1, td1), lambda: None, lambda c: None,
    )
    gen[own, :] = (x0 + out).astype(BF)
    remote(gen.at[own, :], gen.at[own, :], gsend.at[0], grecv.at[0], dev(gg=g_pair))
    for i, ref in enumerate((gd.at[0, :, q_rows, :], xgs.at[:, q_rows, :], hs.at[:, q_rows, :])):
        remote(ref, ref, gsend.at[1 + i], grecv.at[1 + i], dev(gg=g_pair), when=is_late)
    wait_recv(rt, trecv.at[2], off_diag)
    t_row = ct[8:9, :].astype(F32)
    sigma = 0.1 + 0.8 * (t_row[:, 0:1] * 256.0 + t_row[:, EXT : EXT + 1]) / 999.0
    wait_recv(gen.at[pair, :], grecv.at[0])
    remote(gen.at[mine, :], gen.at[mine, :], gsend.at[4], grecv.at[4], dev(gg=g_near))

    gen_f = gen[mine, :].astype(F32)
    x_t = ((1.0 - sigma) * gen_f + sigma * rt[...].astype(F32)).astype(BF).astype(F32)
    all_rows = pl.ds(0, HALF)
    xgf_2 = xgf.at[1, :, :, pl.ds(0, FEAT)]
    hf_2 = lambda c: hf.at[1, :, :, pl.ds(c * HC, HC)]
    near = dev(gg=g_near)
    gain_row = jnp.where(is_late, gain[2:3, :], gain[1:2, :])
    out = forward(
        1, HALF, x_t, gain_row, xgf.at[half], all_rows, hf.at[half], all_rows,
        (sb2, rb2, po2, zs2, zr2, acc2, ta2, tb2, tc2, td2),
        lambda: remote(xgf_2, xgf_2, gsend.at[5], grecv.at[5], near, when=is_2),
        lambda c: remote(hf_2(c), hf_2(c), gsend.at[10 + c], grecv.at[10 + c], near, when=is_2),
    )
    fk[...] = (x_t + out).astype(BF)
    remote(fk, fother, gsend.at[6], grecv.at[6], dev(gg=g_pair), when=is_late)

    scale = 1.0 / math.sqrt(TOKENS)
    dy = dyb.at[half]

    @pl.when(is_late)
    def _():
        dy[t, :, :FEAT] = ((fk[...].astype(F32) - gen_f) * scale).astype(BF)
        dy[t, :, FEAT:] = jnp.zeros((HALF, EXT), BF)

    @pl.when(is_early)
    def _():
        real = fk[...].astype(F32)
        distance = jnp.sum(jnp.sum(jnp.abs(gen_f - real), axis=1, keepdims=True), axis=0, keepdims=True)
        dmine[0] = jnp.broadcast_to(distance, (8, EXT))
        cp = pltpu.make_async_remote_copy(
            src_ref=dmine.at[0], dst_ref=dmine.at[1], send_sem=gsend.at[7], recv_sem=grecv.at[7],
            device_id=near, device_id_type=MESH,
        )
        cp.start()
        wait_recv(fother, grecv.at[6])
        dy[t, :, :FEAT] = ((fother[...].astype(F32) - real) * scale).astype(BF)
        cp.wait()
        both = jnp.broadcast_to(dmine[0, 0:1, 0:1] + dmine[1, 0:1, 0:1], (HALF, 1))
        dy[t, :, FEAT:] = split_scalar(both).astype(BF)

    dy_block = lambda b: dy.at[b]
    gather_tp(2, dy_block)

    wait_recv(gen.at[other, :], grecv.at[4])
    remote(gen, gout, tsend.at[3], trecv.at[3], flip, when=off_diag)

    da = dab.at[half]
    back = dnw.at[late]
    slope = gd.at[late]

    def product(rows, c):
        return lax.dot_general(
            rows, back[c * HC : (c + 1) * HC, :], (((1,), (1,)), ((), ())), preferred_element_type=F32
        )

    def da_piece(buf, yy, c):
        start, width = wide_cols(c)
        return buf.at[pl.ds(2 * yy, 2), :, pl.ds(start, width)]

    wait_recv(gd.at[0, :, pl.ds(QUARTER, QUARTER), :], grecv.at[1], is_early)
    not_2 = g != 2
    facing = lax.rem(y + 2, 4)
    da_2 = dab.at[1]

    def pass_on(c):
        wait_recv(da_piece(da_2, facing, c), h_r.at[2, c, facing], is_2)
        remote(
            da_piece(da_2, facing, c), da_piece(da_2, facing, c), xs_s.at[c, 1], xs_r.at[c, facing], near, when=is_2
        )
        wait_recv(da_piece(da_2, y, c), xs_r.at[c, y], is_3)
        for j in (1, 3):
            remote(
                da_piece(da_2, y, c), da_piece(da_2, y, c), xs_s.at[c, 1 + j], xs_r.at[c, y],
                row_peer(lax.rem(y + j, 4)), when=is_3,
            )

    def finish(c, dh, distance):
        norm = distance * (1.0 / (IMG_TOK * D_ALL)) + 1e-5
        row_scale = jnp.where(is_late, 1.0, 1.0 / norm)
        start, width = wide_cols(c)
        lo = EXT + c * HC
        two = pl.ds(2 * y, 2)
        if c == 0:
            da[two, :, :EXT] = split_scalar(row_scale).astype(BF).reshape(2, HALF, EXT)
        slopes = slope[:, :, c * HC : (c + 1) * HC].reshape(2 * HALF, HC).astype(F32)
        da[two, :, lo : lo + HC] = (dh * row_scale * slopes).astype(BF).reshape(2, HALF, HC)
        own_piece = da_piece(da, y, c)
        remote(own_piece, own_piece, xs_s.at[c, 0], xs_r.at[c, y], near, when=is_2)
        for j in (2, 1, 3):
            remote(
                own_piece, own_piece, hy_s.at[2, c, j], h_r.at[2, c, y], row_peer(lax.rem(y + j, 4)),
                when=None if j == 2 else not_2,
            )
        if c:
            pass_on(c - 1)

    dyb_2 = dyb.at[1, :, :, pl.ds(0, FEAT)]
    reduce_rep(
        2, HALF, lambda yy: dy[pl.ds(2 * yy, 2)].reshape(2 * HALF, ROW), dy_block, product,
        (sb3, rb3, po3, zs3, zr3), finish,
        lambda: remote(dyb_2, dyb_2, gsend.at[8], grecv.at[8], near, when=is_2),
    )
    pass_on(CHUNKS - 1)

    for i, ref in enumerate((xgs.at[:, pl.ds(QUARTER, QUARTER), :], hs.at[:, pl.ds(QUARTER, QUARTER), :])):
        wait_recv(ref, grecv.at[2 + i], is_early)
    wait_recv(xgf_2, grecv.at[5], is_3)
    for c in range(CHUNKS):
        wait_recv(hf_2(c), grecv.at[10 + c], is_3)
    wait_recv(dyb_2, grecv.at[8], is_3)

    tn = (((0,), (0,)), ((), ()))
    step = 256

    def up_grad(u_of, da_of):
        def tile(i, _):
            cols = pl.ds(pl.multiple_of(i * step, step), step)
            wide = pl.ds(pl.multiple_of(EXT + i * step, EXT), step)
            upg_out[:, cols] = lax.dot_general(u_of(), da_of(wide), tn, preferred_element_type=F32).astype(BF)
            return 0

        lax.fori_loop(0, HID // step, tile, 0)

    def down_grad(h_of, upstream):
        def tile(i, _):
            cols = pl.ds(pl.multiple_of(i * step, step), step)
            dng_out[cols, :] = lax.dot_general(h_of(cols), upstream, tn, preferred_element_type=F32).astype(BF)
            return 0

        lax.fori_loop(0, HID // step, tile, 0)

    n_half, n_all = BLOCKS * HALF, 2 * BLOCKS * HALF

    @pl.when(is_2)
    def _():
        upg_out[...] = jnp.zeros_like(upg_out)
        dng_out[...] = jnp.zeros_like(dng_out)

    @pl.when(is_3)
    def _():
        down_grad(lambda cols: hf[:, :, :, cols].reshape(n_all, -1), dyb[:, :, :, :FEAT].reshape(n_all, FEAT))

    for c in range(CHUNKS):
        for j in (1, 3, 2):
            yy = lax.rem(y + j, 4)
            wait_recv(da_piece(da, yy, c), h_r.at[2, c, yy], not_2)
            wait_recv(da_piece(da_2, yy, c), xs_r.at[c, yy], is_3)

    @pl.when(is_early)
    def _():
        row_scale = join_scalar(da[:, :, :EXT].reshape(n_half, EXT).astype(F32))
        upstream = (dy[:, :, :FEAT].reshape(n_half, FEAT).astype(F32) * row_scale).astype(BF)
        down_grad(lambda cols: hs[:, :, cols].reshape(n_half, -1), upstream)
        up_grad(lambda: xgs[:, :, :FEAT].reshape(n_half, FEAT), lambda cols: da[:, :, cols].reshape(n_half, -1))

    @pl.when(is_3)
    def _():
        up_grad(
            lambda: xgf[:, :, :, :FEAT].reshape(n_all, FEAT), lambda cols: dab[:, :, :, cols].reshape(n_all, -1)
        )

    wait_recv(gout, trecv.at[3], off_diag)

    @pl.when(off_diag)
    def _():
        gen_out[...] = gout[...].astype(F32)

    @pl.when(jnp.logical_not(off_diag))
    def _():
        gen_out[...] = gen[...].astype(F32)

    for cp, when in sends:
        if when is None:
            cp.wait_send()
        else:
            pl.when(when)(cp.wait_send)


def rep_buffers(n):
    return [
        pltpu.VMEM((4, 2 * n, WIDE), BF),
        pltpu.VMEM((4, 2 * n, WIDE), BF),
        pltpu.VMEM((2 * n, WIDE), F32),
        pltpu.VMEM((2 * n, WIDE), BF),
        pltpu.VMEM((2 * n, WIDE), BF),
    ]


def tp_buffers(n):
    return [
        pltpu.VMEM((BLOCKS, n, FEAT), F32),
        pltpu.VMEM((4, n, FEAT), BF),
        pltpu.VMEM((4, n, FEAT), BF),
        pltpu.VMEM((3, n, FEAT), BF),
        pltpu.VMEM((3, n, FEAT), BF),
    ]


def body(noise_in, noise_renoise, text_cond, t_index, gains, up_weights, down_weights):
    vmem = pl.BlockSpec(memory_space=pltpu.VMEM)
    smem = pl.BlockSpec(memory_space=pltpu.SMEM)
    hbm = pl.BlockSpec(memory_space=pl.ANY)
    dma = pltpu.SemaphoreType.DMA
    generated, up_grad, down_grad = pl.pallas_call(
        kernel,
        name="step",
        out_shape=(
            jax.ShapeDtypeStruct((IMG_TOK, FEAT), F32),
            jax.ShapeDtypeStruct((FEAT, HID), BF),
            jax.ShapeDtypeStruct((HID, FEAT), BF),
        ),
        in_specs=[vmem, vmem, vmem, smem, vmem, hbm, hbm],
        out_specs=(vmem, vmem, vmem),
        scratch_shapes=[
            pltpu.VMEM((16, FEAT), BF),
            pltpu.VMEM((QUARTER, FEAT), BF),
            pltpu.VMEM((16, FEAT), BF),
            pltpu.VMEM((HALF, FEAT), BF),
            pltpu.VMEM((IMG_TOK, FEAT), BF),
            pltpu.VMEM((IMG_TOK, FEAT), BF),
            pltpu.VMEM((HALF, FEAT), BF),
            pltpu.VMEM((HALF, FEAT), BF),
            pltpu.VMEM((2, 8, EXT), F32),
            pltpu.VMEM((2, FEAT, HID), BF),
            pltpu.VMEM((2, HID, FEAT), BF),
            pltpu.VMEM((BLOCKS, HALF, ROW), BF),
            pltpu.VMEM((BLOCKS, HALF, HID), BF),
            pltpu.VMEM((2, BLOCKS, HALF, ROW), BF),
            pltpu.VMEM((2, BLOCKS, HALF, HID), BF),
            pltpu.VMEM((2, BLOCKS, HALF, ROW), BF),
            pltpu.VMEM((2, BLOCKS, HALF, WIDE), BF),
            pltpu.VMEM((2, 2, HALF, HID), BF),
            *rep_buffers(QUARTER),
            *tp_buffers(QUARTER),
            *rep_buffers(HALF),
            *tp_buffers(HALF),
            *rep_buffers(HALF),
            dma((4,)),
            dma((4,)),
            dma((4,)),
            dma((10 + CHUNKS,)),
            dma((10 + CHUNKS,)),
            dma((3, 7)),
            dma((3, 8)),
            dma((3, CHUNKS, 4)),
            dma((3, CHUNKS, 4)),
            dma((3, CHUNKS)),
            dma((3, CHUNKS)),
            dma((3, CHUNKS, 4)),
            dma((3, CHUNKS, 4)),
            dma((2, 7)),
            dma((2, 7)),
            dma((CHUNKS, 5)),
            dma((CHUNKS, 4)),
        ],
        compiler_params=pltpu.CompilerParams(
            collective_id=0, has_side_effects=True, vmem_limit_bytes=60 * 2**20
        ),
    )(noise_in, noise_renoise, text_cond, t_index, gains, up_weights, down_weights)
    return generated.astype(BF), up_grad.astype(F32)[None], down_grad.astype(F32)[None]


def solution(mesh):
    in_specs = (
        P("rep", "tp"),
        P("rep", "tp"),
        P("rep", None),
        P("rep"),
        P(),
        P(None, "rep", "tp"),
        P(None, "tp", "rep"),
    )
    out_specs = (P("rep", "tp"), P("grp", "rep", "tp"), P("grp", "tp", "rep"))
    return jax.shard_map(body, mesh=mesh, in_specs=in_specs, out_specs=out_specs, check_vma=False)
```

time: 253 us -> 181 us (0.72)
  the two profiles are of different devices: /device:TPU:1 before, /device:TPU:102 now
where the time goes in v2:
time: 181 us; the launch traced here: 180 us
  Pallas kernels  172 us (95%)
  other arithmetic  6.2 us (3%)
    pallas_call x1, Pallas kernels, body(): pl.pallas_call(kernel, name='step', out_shape=(jax.ShapeDtypeStruct((IMG_...  172 us

profile of v2, /device:TPU:102, one launch (start us, length us, event | category | flops | bytes accessed | tf_op | source)
XLA Modules:
  0.0 179.6 jit_solution(5567002302182494191)
XLA Ops:
  1.3 172.1 %step.1 = (f32[128,384]{1,0:T(8,128)}, bf16[384,1536]{1,0:T(8,128)(2,1)}, bf16[1536,384]{1,0:T(8,128)(2,1)}) custom-call(bf16[128,384]{1,0:T(8,128)(2,1)} %noise.1, bf16[128,384]{1,0:T(8,128)(2,1)} %renoise.1, bf16[1,3072]{1,0:T(2,128)(2,1)} %cond_in.1, s32[1]{0:T(128)S(6)} %copy.10.t_in, f32[3,3072]{1,0:T(4,128)} %gains.1, bf16[3,384,1536]{2,1,0:T(8,128)(2,1)} %up_hbm.1, ...), custom_call_target="tpu_custom_call" | custom-call | tf_op jit(solution)/shard_map/step/pallas_call | solution.py:526
  173.4 0.0 copy-start
  173.4 1.7 convert_element_type.2
  175.1 3.0 %bitcast_convert_fusion.1 = f32[1,384,1536]{2,1,0:T(8,128)} fusion(bf16[384,1536]{1,0:T(8,128)(2,1)} %get-tuple-element.7), kind=kLoop, calls=%fused_computation.1 | loop fusion | flops 589824 | bytes 3538944 | tf_op jit(solution)/shard_map/broadcast_in_dim | solution.py:582
  178.0 0.0 copy-done
  178.1 1.6 bitcast_convert_fusion
Async XLA Ops:
  173.4 4.7 %copy-start = (bf16[1536,384]{1,0:T(8,128)(2,1)S(1)}, bf16[1536,384]{1,0:T(8,128)(2,1)}, u32[]{:S(2)}) copy-start(bf16[1536,384]{1,0:T(8,128)(2,1)} %get-tuple-element.8) | copy-start | bytes 3538948

commit v3 on v2

--- a/solution.py
+++ b/solution.py
@@ -13,9 +13,7 @@
 F32 = jnp.float32
 FEAT = 384
 HID = 1536
-EXT = 128
-ROW = FEAT + EXT
-WIDE = EXT + HID
+LANES = 128
 CHUNKS = 4
 HC = HID // CHUNKS
 BLOCKS = 8
@@ -27,15 +25,16 @@
 GELU_C = math.sqrt(2.0 / math.pi)
 
 
-def split_scalar(value):
-    high = value.astype(BF).astype(F32)
-    low = value - high
-    lane = lax.broadcasted_iota(jnp.int32, (value.shape[0], EXT), 1)
-    return jnp.where(lane < EXT // 2, high, low)
-
-
-def join_scalar(columns):
-    return columns[:, 0:1] + columns[:, EXT // 2 : EXT // 2 + 1]
+def diagonal(n):
+    return lax.broadcasted_iota(jnp.int32, (n, LANES), 0) == lax.broadcasted_iota(jnp.int32, (n, LANES), 1)
+
+
+def to_lanes(column):
+    return jnp.sum(jnp.where(diagonal(column.shape[0]), column, 0.0), axis=0, keepdims=True)
+
+
+def to_column(lanes, n):
+    return jnp.sum(jnp.where(diagonal(n), lanes, 0.0), axis=1, keepdims=True)
 
 
 def gelu_both(a):
@@ -46,20 +45,18 @@
     return a * half, grad
 
 
-def wide_cols(c):
-    return (0, EXT + HC) if c == 0 else (EXT + c * HC, HC)
-
-
 def kernel(
     noise, renoise, cond_in, t_in, gains, up_hbm, down_hbm,
     gen_out, upg_out, dng_out,
     msgc, xt, ct, rt, gen, gout, fk, fother, dmine,
-    upw, dnw, xgs, hs, xgf, hf, dyb, dab, gd,
+    upw, dnw, xgs, hs, xgf, hf, dyb, dab, gd, dys, ut,
+    sc_own, sc_row, sc_zs, sc_zr, sc_all,
     sb1, rb1, po1, zs1, zr1, acc1, ta1, tb1, tc1, td1,
     sb2, rb2, po2, zs2, zr2, acc2, ta2, tb2, tc2, td2,
     sb3, rb3, po3, zs3, zr3,
     wsem, tsend, trecv, gsend, grecv,
     ag_s, ag_r, ry_s, ry_r, rz_s, rz_r, hy_s, h_r, tp_s, tp_r, xs_s, xs_r,
+    sy_s, sy_r, sz_s, sz_r, st_s, st_r,
 ):
     g, r, t = lax.axis_index("grp"), lax.axis_index("rep"), lax.axis_index("tp")
     y, zh = lax.div(r, 2), lax.rem(r, 2)
@@ -120,11 +117,11 @@
     for peer in peers:
         pl.semaphore_signal(barrier, inc=1, device_id=peer, device_id_type=MESH)
 
-    cond_row = cond_in[0:1, pl.ds(pl.multiple_of(t * FEAT, EXT), FEAT)].astype(F32)
+    cond_row = cond_in[0:1, pl.ds(pl.multiple_of(t * FEAT, LANES), FEAT)].astype(F32)
     t_all = jnp.full((16, FEAT), t_in[0], jnp.int32)
     row = lax.broadcasted_iota(jnp.int32, (16, FEAT), 0)
     lane = lax.broadcasted_iota(jnp.int32, (16, FEAT), 1)
-    t_part = jnp.where(lane < EXT, t_all >> 8, t_all & 255).astype(F32)
+    t_part = jnp.where(lane < LANES, t_all >> 8, t_all & 255).astype(F32)
     msgc[...] = jnp.where(row < 8, jnp.broadcast_to(cond_row, (16, FEAT)), t_part).astype(BF)
 
     @pl.when(off_diag)
@@ -169,67 +166,87 @@
         b = 2 * yy + 1 - core
         wait_recv(block_of(b), ag_r.at[phase, b])
 
+    def scalar_start(phase, lanes):
+        sc_own[phase] = jnp.broadcast_to(lanes, (8, LANES))
+        for j in (2, 1, 3):
+            remote(
+                sc_own.at[phase], sc_row.at[phase, y], sy_s.at[phase, j], sy_r.at[phase, y],
+                row_peer(lax.rem(y + j, 4)),
+            )
+
+    def scalar_to_z(phase):
+        total = sc_own[phase]
+        for j in (1, 3, 2):
+            yy = lax.rem(y + j, 4)
+            wait_recv(sc_row.at[phase, yy], sy_r.at[phase, yy])
+            total += sc_row[phase, yy]
+        sc_zs[phase] = total
+        remote(sc_zs.at[phase], sc_zr.at[phase], sz_s.at[phase], sz_r.at[phase], z_peer)
+
+    def scalar_to_tp(phase):
+        wait_recv(sc_zr.at[phase], sz_r.at[phase])
+        sc_all[phase, t] = sc_zs[phase] + sc_zr[phase]
+        tile = sc_all.at[phase, t]
+        remote(tile, tile, st_s.at[phase, 0], st_r.at[phase, t], sibling)
+        for d in (2, 1, 3):
+            remote(tile, tile, st_s.at[phase, d], st_r.at[phase, t], dev(tt=2 * lax.rem(zl + d, 4) + core))
+
+    def scalar_end(phase):
+        for d in (1, 3, 2):
+            b = 2 * lax.rem(zl + d, 4) + core
+            tile = sc_all.at[phase, b]
+            wait_recv(tile, st_r.at[phase, b])
+            remote(tile, tile, st_s.at[phase, 3 + d], st_r.at[phase, b], sibling)
+        for d in range(4):
+            b = 2 * lax.rem(zl + d, 4) + 1 - core
+            wait_recv(sc_all.at[phase, b], st_r.at[phase, b])
+
     def reduce_rep(phase, n, rows_of, block_of, product, bufs, finish, gathered):
         sb, rb, po, zs, zr = bufs
+        span = lambda c: pl.ds(c * HC, HC)
         for c in range(CHUNKS):
-            start, width = wide_cols(c)
-            lo = EXT + c * HC
+            lo = c * HC
             for d in (0, 1, 3, 2):
                 yy = lax.rem(zl + d, 4)
                 if c == 0:
                     wait_chip(phase, block_of, d)
-                rows = rows_of(yy)
-                part = product(rows[:, :FEAT], c)
+                part = product(rows_of(yy), c)
 
                 @pl.when(yy == y)
                 def _():
-                    if c == 0:
-                        po[:, :EXT] = rows[:, FEAT:].astype(F32)
                     po[:, lo : lo + HC] = part
 
                 @pl.when(yy != y)
                 def _():
-                    if c == 0:
-                        sb[yy, :, :EXT] = rows[:, FEAT:]
                     sb[yy, :, lo : lo + HC] = part.astype(BF)
 
-                cols = pl.ds(start, width)
                 remote(
-                    sb.at[yy, :, cols], rb.at[y, :, cols], ry_s.at[phase, c, d], ry_r.at[phase, c, y],
+                    sb.at[yy, :, span(c)], rb.at[y, :, span(c)], ry_s.at[phase, c, d], ry_r.at[phase, c, y],
                     row_peer(yy), when=yy != y,
                 )
+                if c == 0 and d == 0:
+                    scalar_to_z(phase)
             if c == 0:
                 gathered()
+        scalar_to_tp(phase)
 
         def to_z(c):
-            start, width = wide_cols(c)
-            others = [lax.rem(y + j, 4) for j in (1, 3, 2)]
-            for yy in others:
-                wait_recv(rb.at[yy, :, pl.ds(start, width)], ry_r.at[phase, c, yy])
-
-            def add_up(lo, wid):
-                total = po[:, lo : lo + wid]
-                for yy in others:
-                    total += rb[yy, :, lo : lo + wid].astype(F32)
-                po[:, lo : lo + wid] = total
-                return total
-
+            lo = c * HC
+            total = po[:, lo : lo + HC]
+            for j in (1, 3, 2):
+                yy = lax.rem(y + j, 4)
+                wait_recv(rb.at[yy, :, span(c)], ry_r.at[phase, c, yy])
+                total += rb[yy, :, lo : lo + HC].astype(F32)
+            po[:, lo : lo + HC] = total
+            zs[:, lo : lo + HC] = total.astype(BF)
+            remote(zs.at[:, span(c)], zr.at[:, span(c)], rz_s.at[phase, c], rz_r.at[phase, c], z_peer)
+
+        def from_z(c):
+            lo = c * HC
             if c == 0:
-                zs[:, :EXT] = split_scalar(join_scalar(add_up(0, EXT))).astype(BF)
-            lo = EXT + c * HC
-            zs[:, lo : lo + HC] = add_up(lo, HC).astype(BF)
-            cols = pl.ds(start, width)
-            remote(zs.at[:, cols], zr.at[:, cols], rz_s.at[phase, c], rz_r.at[phase, c], z_peer)
-
-        state = {}
-
-        def from_z(c):
-            start, width = wide_cols(c)
-            wait_recv(zr.at[:, pl.ds(start, width)], rz_r.at[phase, c])
-            if c == 0:
-                state["scalar"] = join_scalar(po[:, :EXT] + zr[:, :EXT].astype(F32))
-            lo = EXT + c * HC
-            finish(c, po[:, lo : lo + HC] + zr[:, lo : lo + HC].astype(F32), state["scalar"])
+                scalar_end(phase)
+            wait_recv(zr.at[:, span(c)], rz_r.at[phase, c])
+            finish(c, po[:, lo : lo + HC] + zr[:, lo : lo + HC].astype(F32))
 
         ahead = CHUNKS - 1 if n == HALF else CHUNKS
         for c in range(CHUNKS):
@@ -242,11 +259,11 @@
     def forward(phase, n, x_rows, gain_row, xg, xg_rows, h, h_rows, bufs, gathered, chunk_here):
         acc, ta, tb, tc, td = bufs[5:]
         up, down, grad = upw.at[phase], dnw.at[phase], gd.at[phase]
-        xg[t, xg_rows, :FEAT] = (x_rows * (gain_row * cond1)).astype(BF)
-        xg[t, xg_rows, FEAT:] = split_scalar(jnp.sum(x_rows * x_rows, axis=1, keepdims=True)).astype(BF)
+        xg[t, xg_rows, :] = (x_rows * (gain_row * cond1)).astype(BF)
         block_of = lambda b: xg.at[b, xg_rows, :]
         gather_tp(phase, block_of)
-        rows_of = lambda yy: xg[pl.ds(2 * yy, 2), xg_rows, :].reshape(2 * n, ROW)
+        scalar_start(phase, to_lanes(jnp.sum(x_rows * x_rows, axis=1, keepdims=True)))
+        rows_of = lambda yy: xg[pl.ds(2 * yy, 2), xg_rows, :].reshape(2 * n, FEAT)
         loads[2 * phase].wait()
 
         def product(rows, c):
@@ -254,8 +271,13 @@
 
         piece = lambda yy, c: h.at[pl.ds(2 * yy, 2), h_rows, pl.ds(c * HC, HC)]
 
-        def finish(c, a, square_sum):
-            factor = lax.rsqrt(square_sum * (1.0 / D_ALL) + 1e-6)
+        state = {}
+
+        def finish(c, a):
+            if c == 0:
+                squares = [to_column(sc_all[phase, 2 * y + k, 0:1, :], n) for k in range(2)]
+                state["factor"] = lax.rsqrt(jnp.concatenate(squares, axis=0) * (1.0 / D_ALL) + 1e-6)
+            factor = state["factor"]
             hidden, slope = gelu_both(a * factor)
             cols = slice(c * HC, (c + 1) * HC)
             h[pl.ds(2 * y, 2), h_rows, cols] = hidden.astype(BF).reshape(2, n, HC)
@@ -277,19 +299,17 @@
                 both = h[pl.ds(2 * yy, 2), h_rows, cols].reshape(2 * n, HC)
                 part = jnp.dot(both, down[cols, :], preferred_element_type=F32).reshape(2, n, FEAT)
                 if c:
-                    acc[pl.ds(2 * yy, 2)] += part
-                else:
-                    acc[pl.ds(2 * yy, 2)] = part
+                    part += acc[pl.ds(2 * yy, 2)]
+                acc[pl.ds(2 * yy, 2)] = part
+                if c == CHUNKS - 1:
+                    ta[yy] = acc[2 * yy + 1 - core].astype(BF)
+                    remote(ta.at[yy], tb.at[yy], tp_s.at[phase, yy], tp_r.at[phase, yy], sibling)
             chunk_here(c)
-        for d in (2, 1, 3, 0):
-            yy = lax.rem(zl + d, 4)
-            ta[d] = acc[2 * yy + 1 - core].astype(BF)
-            remote(ta.at[d], tb.at[d], tp_s.at[phase, d], tp_r.at[phase, d], sibling)
         total = None
         for d in (2, 1, 3, 0):
             yy = lax.rem(zl + d, 4)
-            wait_recv(tb.at[d], tp_r.at[phase, d])
-            both = acc[2 * yy + core] + tb[d].astype(F32)
+            wait_recv(tb.at[yy], tp_r.at[phase, yy])
+            both = acc[2 * yy + core] + tb[yy].astype(F32)
             if d:
                 tc[d - 1] = both.astype(BF)
                 remote(
@@ -303,7 +323,7 @@
             total += td[d - 1].astype(F32)
         return total
 
-    gain = gains[:, pl.ds(pl.multiple_of(r * FEAT, EXT), FEAT)]
+    gain = gains[:, pl.ds(pl.multiple_of(r * FEAT, LANES), FEAT)]
     x0 = xt[...].astype(F32)
     q_rows = pl.ds(qrow, QUARTER)
     out = forward(
@@ -316,21 +336,27 @@
         remote(ref, ref, gsend.at[1 + i], grecv.at[1 + i], dev(gg=g_pair), when=is_late)
     wait_recv(rt, trecv.at[2], off_diag)
     t_row = ct[8:9, :].astype(F32)
-    sigma = 0.1 + 0.8 * (t_row[:, 0:1] * 256.0 + t_row[:, EXT : EXT + 1]) / 999.0
+    sigma = 0.1 + 0.8 * (t_row[:, 0:1] * 256.0 + t_row[:, LANES : LANES + 1]) / 999.0
     wait_recv(gen.at[pair, :], grecv.at[0])
     remote(gen.at[mine, :], gen.at[mine, :], gsend.at[4], grecv.at[4], dev(gg=g_near))
 
     gen_f = gen[mine, :].astype(F32)
     x_t = ((1.0 - sigma) * gen_f + sigma * rt[...].astype(F32)).astype(BF).astype(F32)
     all_rows = pl.ds(0, HALF)
-    xgf_2 = xgf.at[1, :, :, pl.ds(0, FEAT)]
+    xgf_2 = xgf.at[1]
     hf_2 = lambda c: hf.at[1, :, :, pl.ds(c * HC, HC)]
     near = dev(gg=g_near)
+
+    def inputs_here():
+        wait_recv(gen.at[other, :], grecv.at[4])
+        remote(gen, gout, tsend.at[3], trecv.at[3], flip, when=off_diag)
+        remote(xgf_2, xgf_2, gsend.at[5], grecv.at[5], near, when=is_2)
+
     gain_row = jnp.where(is_late, gain[2:3, :], gain[1:2, :])
     out = forward(
         1, HALF, x_t, gain_row, xgf.at[half], all_rows, hf.at[half], all_rows,
         (sb2, rb2, po2, zs2, zr2, acc2, ta2, tb2, tc2, td2),
-        lambda: remote(xgf_2, xgf_2, gsend.at[5], grecv.at[5], near, when=is_2),
+        inputs_here,
         lambda c: remote(hf_2(c), hf_2(c), gsend.at[10 + c], grecv.at[10 + c], near, when=is_2),
     )
     fk[...] = (x_t + out).astype(BF)
@@ -341,30 +367,26 @@
 
     @pl.when(is_late)
     def _():
-        dy[t, :, :FEAT] = ((fk[...].astype(F32) - gen_f) * scale).astype(BF)
-        dy[t, :, FEAT:] = jnp.zeros((HALF, EXT), BF)
+        dy[t] = ((fk[...].astype(F32) - gen_f) * scale).astype(BF)
+        dmine[...] = jnp.zeros_like(dmine)
 
     @pl.when(is_early)
     def _():
         real = fk[...].astype(F32)
         distance = jnp.sum(jnp.sum(jnp.abs(gen_f - real), axis=1, keepdims=True), axis=0, keepdims=True)
-        dmine[0] = jnp.broadcast_to(distance, (8, EXT))
+        dmine[0] = jnp.broadcast_to(distance, (8, LANES))
         cp = pltpu.make_async_remote_copy(
             src_ref=dmine.at[0], dst_ref=dmine.at[1], send_sem=gsend.at[7], recv_sem=grecv.at[7],
             device_id=near, device_id_type=MESH,
         )
         cp.start()
         wait_recv(fother, grecv.at[6])
-        dy[t, :, :FEAT] = ((fother[...].astype(F32) - real) * scale).astype(BF)
+        dy[t] = ((fother[...].astype(F32) - real) * scale).astype(BF)
         cp.wait()
-        both = jnp.broadcast_to(dmine[0, 0:1, 0:1] + dmine[1, 0:1, 0:1], (HALF, 1))
-        dy[t, :, FEAT:] = split_scalar(both).astype(BF)
 
     dy_block = lambda b: dy.at[b]
     gather_tp(2, dy_block)
-
-    wait_recv(gen.at[other, :], grecv.at[4])
-    remote(gen, gout, tsend.at[3], trecv.at[3], flip, when=off_diag)
+    scalar_start(2, dmine[0, 0:1, :] + dmine[1, 0:1, :])
 
     da = dab.at[half]
     back = dnw.at[late]
@@ -376,8 +398,11 @@
         )
 
     def da_piece(buf, yy, c):
-        start, width = wide_cols(c)
-        return buf.at[pl.ds(2 * yy, 2), :, pl.ds(start, width)]
+        return buf.at[pl.ds(2 * yy, 2), :, pl.ds(c * HC, HC)]
+
+    def image_scale(b):
+        norm = sc_all[2, b, 0:1, 0:1] * (1.0 / (IMG_TOK * D_ALL)) + 1e-5
+        return jnp.where(is_late, 1.0, 1.0 / norm)
 
     wait_recv(gd.at[0, :, pl.ds(QUARTER, QUARTER), :], grecv.at[1], is_early)
     not_2 = g != 2
@@ -385,6 +410,10 @@
     da_2 = dab.at[1]
 
     def pass_on(c):
+        behind, ahead = lax.rem(y + (1 if c % 2 else 3), 4), lax.rem(y + (3 if c % 2 else 1), 4)
+        passed = da_piece(da, behind, c)
+        wait_recv(passed, h_r.at[2, c, behind], not_2)
+        remote(passed, passed, hy_s.at[2, c, 0], h_r.at[2, c, behind], row_peer(ahead), when=not_2)
         wait_recv(da_piece(da_2, facing, c), h_r.at[2, c, facing], is_2)
         remote(
             da_piece(da_2, facing, c), da_piece(da_2, facing, c), xs_s.at[c, 1], xs_r.at[c, facing], near, when=is_2
@@ -396,29 +425,28 @@
                 row_peer(lax.rem(y + j, 4)), when=is_3,
             )
 
-    def finish(c, dh, distance):
-        norm = distance * (1.0 / (IMG_TOK * D_ALL)) + 1e-5
-        row_scale = jnp.where(is_late, 1.0, 1.0 / norm)
-        start, width = wide_cols(c)
-        lo = EXT + c * HC
-        two = pl.ds(2 * y, 2)
+    row_state = {}
+
+    def finish(c, dh):
         if c == 0:
-            da[two, :, :EXT] = split_scalar(row_scale).astype(BF).reshape(2, HALF, EXT)
-        slopes = slope[:, :, c * HC : (c + 1) * HC].reshape(2 * HALF, HC).astype(F32)
-        da[two, :, lo : lo + HC] = (dh * row_scale * slopes).astype(BF).reshape(2, HALF, HC)
+            scales = [jnp.broadcast_to(image_scale(2 * y + k), (HALF, 1)) for k in range(2)]
+            row_state["scale"] = jnp.concatenate(scales, axis=0)
+        cols = slice(c * HC, (c + 1) * HC)
+        slopes = slope[:, :, cols].reshape(2 * HALF, HC).astype(F32)
+        da[pl.ds(2 * y, 2), :, cols] = (dh * row_state["scale"] * slopes).astype(BF).reshape(2, HALF, HC)
         own_piece = da_piece(da, y, c)
         remote(own_piece, own_piece, xs_s.at[c, 0], xs_r.at[c, y], near, when=is_2)
         for j in (2, 1, 3):
             remote(
                 own_piece, own_piece, hy_s.at[2, c, j], h_r.at[2, c, y], row_peer(lax.rem(y + j, 4)),
-                when=None if j == 2 else not_2,
+                when=is_2 if j == 2 else not_2,
             )
         if c:
             pass_on(c - 1)
 
-    dyb_2 = dyb.at[1, :, :, pl.ds(0, FEAT)]
+    dyb_2 = dyb.at[1]
     reduce_rep(
-        2, HALF, lambda yy: dy[pl.ds(2 * yy, 2)].reshape(2 * HALF, ROW), dy_block, product,
+        2, HALF, lambda yy: dy[pl.ds(2 * yy, 2)].reshape(2 * HALF, FEAT), dy_block, product,
         (sb3, rb3, po3, zs3, zr3), finish,
         lambda: remote(dyb_2, dyb_2, gsend.at[8], grecv.at[8], near, when=is_2),
     )
@@ -434,19 +462,10 @@
     tn = (((0,), (0,)), ((), ()))
     step = 256
 
-    def up_grad(u_of, da_of):
+    def down_grad(h_of, upstream_of):
         def tile(i, _):
             cols = pl.ds(pl.multiple_of(i * step, step), step)
-            wide = pl.ds(pl.multiple_of(EXT + i * step, EXT), step)
-            upg_out[:, cols] = lax.dot_general(u_of(), da_of(wide), tn, preferred_element_type=F32).astype(BF)
-            return 0
-
-        lax.fori_loop(0, HID // step, tile, 0)
-
-    def down_grad(h_of, upstream):
-        def tile(i, _):
-            cols = pl.ds(pl.multiple_of(i * step, step), step)
-            dng_out[cols, :] = lax.dot_general(h_of(cols), upstream, tn, preferred_element_type=F32).astype(BF)
+            dng_out[cols, :] = lax.dot_general(h_of(cols), upstream_of(), tn, preferred_element_type=F32).astype(BF)
             return 0
 
         lax.fori_loop(0, HID // step, tile, 0)
@@ -458,28 +477,41 @@
         upg_out[...] = jnp.zeros_like(upg_out)
         dng_out[...] = jnp.zeros_like(dng_out)
 
+    @pl.when(is_early)
+    def _():
+        for k in range(BLOCKS // 2):
+            two = xgs[2 * k : 2 * k + 2].reshape(2 * HALF, FEAT)
+            ut[:, k * LANES : (k + 1) * LANES] = two.T
+        for b in range(BLOCKS):
+            dys[b] = (dy[b].astype(F32) * image_scale(b)).astype(BF)
+        down_grad(lambda cols: hs[:, :, cols].reshape(n_half, -1), lambda: dys[...].reshape(n_half, FEAT))
+
     @pl.when(is_3)
     def _():
-        down_grad(lambda cols: hf[:, :, :, cols].reshape(n_all, -1), dyb[:, :, :, :FEAT].reshape(n_all, FEAT))
+        for k in range(BLOCKS):
+            two = xgf[k // 4, 2 * (k % 4) : 2 * (k % 4) + 2].reshape(2 * HALF, FEAT)
+            ut[:, k * LANES : (k + 1) * LANES] = two.T
+        down_grad(lambda cols: hf[:, :, :, cols].reshape(n_all, -1), lambda: dyb[...].reshape(n_all, FEAT))
 
     for c in range(CHUNKS):
+        cols = slice(c * HC, (c + 1) * HC)
         for j in (1, 3, 2):
             yy = lax.rem(y + j, 4)
-            wait_recv(da_piece(da, yy, c), h_r.at[2, c, yy], not_2)
+            if j != (1 if c % 2 else 3):
+                wait_recv(da_piece(da, yy, c), h_r.at[2, c, yy], not_2)
             wait_recv(da_piece(da_2, yy, c), xs_r.at[c, yy], is_3)
 
-    @pl.when(is_early)
-    def _():
-        row_scale = join_scalar(da[:, :, :EXT].reshape(n_half, EXT).astype(F32))
-        upstream = (dy[:, :, :FEAT].reshape(n_half, FEAT).astype(F32) * row_scale).astype(BF)
-        down_grad(lambda cols: hs[:, :, cols].reshape(n_half, -1), upstream)
-        up_grad(lambda: xgs[:, :, :FEAT].reshape(n_half, FEAT), lambda cols: da[:, :, cols].reshape(n_half, -1))
-
-    @pl.when(is_3)
-    def _():
-        up_grad(
-            lambda: xgf[:, :, :, :FEAT].reshape(n_all, FEAT), lambda cols: dab[:, :, :, cols].reshape(n_all, -1)
-        )
+        @pl.when(is_early)
+        def _():
+            upg_out[:, cols] = jnp.dot(
+                ut[:, :n_half], da[:, :, cols].reshape(n_half, HC), preferred_element_type=F32
+            ).astype(BF)
+
+        @pl.when(is_3)
+        def _():
+            upg_out[:, cols] = jnp.dot(
+                ut[...], dab[:, :, :, cols].reshape(n_all, HC), preferred_element_type=F32
+            ).astype(BF)
 
     wait_recv(gout, trecv.at[3], off_diag)
 
@@ -500,11 +532,11 @@
 
 def rep_buffers(n):
     return [
-        pltpu.VMEM((4, 2 * n, WIDE), BF),
-        pltpu.VMEM((4, 2 * n, WIDE), BF),
-        pltpu.VMEM((2 * n, WIDE), F32),
-        pltpu.VMEM((2 * n, WIDE), BF),
-        pltpu.VMEM((2 * n, WIDE), BF),
+        pltpu.VMEM((4, 2 * n, HID), BF),
+        pltpu.VMEM((4, 2 * n, HID), BF),
+        pltpu.VMEM((2 * n, HID), F32),
+        pltpu.VMEM((2 * n, HID), BF),
+        pltpu.VMEM((2 * n, HID), BF),
     ]
 
 
@@ -542,16 +574,23 @@
             pltpu.VMEM((IMG_TOK, FEAT), BF),
             pltpu.VMEM((HALF, FEAT), BF),
             pltpu.VMEM((HALF, FEAT), BF),
-            pltpu.VMEM((2, 8, EXT), F32),
+            pltpu.VMEM((2, 8, LANES), F32),
             pltpu.VMEM((2, FEAT, HID), BF),
             pltpu.VMEM((2, HID, FEAT), BF),
-            pltpu.VMEM((BLOCKS, HALF, ROW), BF),
+            pltpu.VMEM((BLOCKS, HALF, FEAT), BF),
             pltpu.VMEM((BLOCKS, HALF, HID), BF),
-            pltpu.VMEM((2, BLOCKS, HALF, ROW), BF),
+            pltpu.VMEM((2, BLOCKS, HALF, FEAT), BF),
             pltpu.VMEM((2, BLOCKS, HALF, HID), BF),
-            pltpu.VMEM((2, BLOCKS, HALF, ROW), BF),
-            pltpu.VMEM((2, BLOCKS, HALF, WIDE), BF),
+            pltpu.VMEM((2, BLOCKS, HALF, FEAT), BF),
+            pltpu.VMEM((2, BLOCKS, HALF, HID), BF),
             pltpu.VMEM((2, 2, HALF, HID), BF),
+            pltpu.VMEM((BLOCKS, HALF, FEAT), BF),
+            pltpu.VMEM((FEAT, 2 * BLOCKS * HALF), BF),
+            pltpu.VMEM((3, 8, LANES), F32),
+            pltpu.VMEM((3, 4, 8, LANES), F32),
+            pltpu.VMEM((3, 8, LANES), F32),
+            pltpu.VMEM((3, 8, LANES), F32),
+            pltpu.VMEM((3, BLOCKS, 8, LANES), F32),
             *rep_buffers(QUARTER),
             *tp_buffers(QUARTER),
             *rep_buffers(HALF),
@@ -574,6 +613,12 @@
             dma((2, 7)),
             dma((CHUNKS, 5)),
             dma((CHUNKS, 4)),
+            dma((3, 4)),
+            dma((3, 4)),
+            dma((3,)),
+            dma((3,)),
+            dma((3, 7)),
+            dma((3, 8)),
         ],
         compiler_params=pltpu.CompilerParams(
             collective_id=0, has_side_effects=True, vmem_limit_bytes=60 * 2**20

time: 181 us -> 170 us (0.939)
  Pallas kernels: 172 us -> 160 us
    pallas_call x1, Pallas kernels: 172 us -> 160 us  [body(): pl.pallas_call(kernel, name='step', out_shape=(jax.ShapeDtypeStruct((IMG_...]
where the time goes in v3:
time: 170 us; the launch traced here: 168 us
  Pallas kernels  160 us (94%)
  other arithmetic  6.2 us (4%)
    pallas_call x1, Pallas kernels, body(): pl.pallas_call(kernel, name='step', out_shape=(jax.ShapeDtypeStruct((IMG_...  160 us

profile of v3, /device:TPU:102, one launch (start us, length us, event | category | flops | bytes accessed | tf_op | source)
XLA Modules:
  0.0 167.9 jit_solution(16252149196655558696)
XLA Ops:
  1.3 160.4 %step.1 = (f32[128,384]{1,0:T(8,128)}, bf16[384,1536]{1,0:T(8,128)(2,1)}, bf16[1536,384]{1,0:T(8,128)(2,1)}) custom-call(bf16[128,384]{1,0:T(8,128)(2,1)} %noise.1, bf16[128,384]{1,0:T(8,128)(2,1)} %renoise.1, bf16[1,3072]{1,0:T(2,128)(2,1)} %cond_in.1, s32[1]{0:T(128)S(6)} %copy.10.t_in, f32[3,3072]{1,0:T(4,128)} %gains.1, bf16[3,384,1536]{2,1,0:T(8,128)(2,1)} %up_hbm.1, ...), custom_call_target="tpu_custom_call" | custom-call | tf_op jit(solution)/shard_map/step/pallas_call | solution.py:558
  161.7 0.0 copy-start
  161.7 1.7 convert_element_type.2
  163.4 3.0 %bitcast_convert_fusion.1 = f32[1,384,1536]{2,1,0:T(8,128)} fusion(bf16[384,1536]{1,0:T(8,128)(2,1)} %get-tuple-element.7), kind=kLoop, calls=%fused_computation.1 | loop fusion | flops 589824 | bytes 3538944 | tf_op jit(solution)/shard_map/broadcast_in_dim | solution.py:627
  166.4 0.0 copy-done
  166.4 1.6 bitcast_convert_fusion
Async XLA Ops:
  161.7 4.7 %copy-start = (bf16[1536,384]{1,0:T(8,128)(2,1)S(1)}, bf16[1536,384]{1,0:T(8,128)(2,1)}, u32[]{:S(2)}) copy-start(bf16[1536,384]{1,0:T(8,128)(2,1)} %get-tuple-element.8) | copy-start | bytes 3538948

commit v4 on v3

--- a/solution.py
+++ b/solution.py
@@ -46,8 +46,9 @@
 
 
 def kernel(
-    noise, renoise, cond_in, t_in, gains, up_hbm, down_hbm,
-    gen_out, upg_out, dng_out,
+    noise_hbm, renoise_hbm, cond_in, t_in, gains_hbm, up_hbm, down_hbm,
+    gen_hbm, upg_hbm, dng_hbm,
+    noise, renoise, gain, upg_out, dng_out, isem, osem,
     msgc, xt, ct, rt, gen, gout, fk, fother, dmine,
     upw, dnw, xgs, hs, xgf, hf, dyb, dab, gd, dys, ut,
     sc_own, sc_row, sc_zs, sc_zr, sc_all,
@@ -95,6 +96,16 @@
         else:
             pl.when(when)(cp.wait_recv)
 
+    own = pl.ds(pl.multiple_of(half * HALF + quart * QUARTER, QUARTER), QUARTER)
+    pair = pl.ds(pl.multiple_of(half * HALF + (1 - quart) * QUARTER, QUARTER), QUARTER)
+    mine = pl.ds(pl.multiple_of(half * HALF, HALF), HALF)
+    other = pl.ds(pl.multiple_of((1 - half) * HALF, HALF), HALF)
+    inputs = [
+        pltpu.make_async_copy(noise_hbm.at[own, :], noise, isem.at[0]),
+        pltpu.make_async_copy(renoise_hbm.at[mine, :], renoise, isem.at[1]),
+        pltpu.make_async_copy(gains_hbm.at[:, pl.ds(pl.multiple_of(r * FEAT, LANES), FEAT)], gain, isem.at[2]),
+    ]
+
     model = 1 + late
     loads = [
         pltpu.make_async_copy(up_hbm.at[0], upw.at[0], wsem.at[0]),
@@ -102,9 +113,6 @@
         pltpu.make_async_copy(up_hbm.at[model], upw.at[1], wsem.at[2]),
         pltpu.make_async_copy(down_hbm.at[model], dnw.at[1], wsem.at[3]),
     ]
-    for cp in loads:
-        cp.start()
-
     barrier = pltpu.get_barrier_semaphore()
     sibling = dev(tt=2 * zl + 1 - core)
     flip = dev(rr=t, tt=r)
@@ -117,6 +125,9 @@
     for peer in peers:
         pl.semaphore_signal(barrier, inc=1, device_id=peer, device_id_type=MESH)
 
+    for cp in inputs + loads:
+        cp.start()
+
     cond_row = cond_in[0:1, pl.ds(pl.multiple_of(t * FEAT, LANES), FEAT)].astype(F32)
     t_all = jnp.full((16, FEAT), t_in[0], jnp.int32)
     row = lax.broadcasted_iota(jnp.int32, (16, FEAT), 0)
@@ -133,19 +144,17 @@
     def _():
         pl.semaphore_wait(barrier, len(peers))
 
-    own = pl.ds(pl.multiple_of(half * HALF + quart * QUARTER, QUARTER), QUARTER)
-    pair = pl.ds(pl.multiple_of(half * HALF + (1 - quart) * QUARTER, QUARTER), QUARTER)
-    mine = pl.ds(pl.multiple_of(half * HALF, HALF), HALF)
-    other = pl.ds(pl.multiple_of((1 - half) * HALF, HALF), HALF)
-    remote(noise.at[own, :], xt, tsend.at[0], trecv.at[0], flip, when=off_diag)
+    for cp in inputs:
+        cp.wait()
+    remote(noise, xt, tsend.at[0], trecv.at[0], flip, when=off_diag)
     remote(msgc, ct, tsend.at[1], trecv.at[1], flip, when=off_diag)
-    remote(renoise.at[mine, :], rt, tsend.at[2], trecv.at[2], flip, when=off_diag)
+    remote(renoise, rt, tsend.at[2], trecv.at[2], flip, when=off_diag)
 
     @pl.when(jnp.logical_not(off_diag))
     def _():
-        xt[...] = noise[own, :]
+        xt[...] = noise[...]
         ct[...] = msgc[...]
-        rt[...] = renoise[mine, :]
+        rt[...] = renoise[...]
 
     wait_recv(xt, trecv.at[0], off_diag)
     wait_recv(ct, trecv.at[1], off_diag)
@@ -224,7 +233,7 @@
                     sb.at[yy, :, span(c)], rb.at[y, :, span(c)], ry_s.at[phase, c, d], ry_r.at[phase, c, y],
                     row_peer(yy), when=yy != y,
                 )
-                if c == 0 and d == 0:
+                if c == 0 and d == 1:
                     scalar_to_z(phase)
             if c == 0:
                 gathered()
@@ -272,6 +281,13 @@
         piece = lambda yy, c: h.at[pl.ds(2 * yy, 2), h_rows, pl.ds(c * HC, HC)]
 
         state = {}
+        relayed = n == HALF
+
+        def pass_on(c):
+            behind, ahead = lax.rem(y + (1 if c % 2 else 3), 4), lax.rem(y + (3 if c % 2 else 1), 4)
+            passed = piece(behind, c)
+            wait_recv(passed, h_r.at[phase, c, behind])
+            remote(passed, passed, hy_s.at[phase, c, 2], h_r.at[phase, c, behind], row_peer(ahead))
 
         def finish(c, a):
             if c == 0:
@@ -281,20 +297,24 @@
             hidden, slope = gelu_both(a * factor)
             cols = slice(c * HC, (c + 1) * HC)
             h[pl.ds(2 * y, 2), h_rows, cols] = hidden.astype(BF).reshape(2, n, HC)
-            for j in (2, 1, 3):
+            for j in (1, 3) if relayed else (2, 1, 3):
                 remote(
                     piece(y, c), piece(y, c), hy_s.at[phase, c, j], h_r.at[phase, c, y],
                     row_peer(lax.rem(y + j, 4)),
                 )
+            if relayed and c:
+                pass_on(c - 1)
             grad[:, h_rows, cols] = (slope * factor).astype(BF).reshape(2, n, HC)
 
         reduce_rep(phase, n, rows_of, block_of, product, bufs[:5], finish, gathered)
+        if relayed:
+            pass_on(CHUNKS - 1)
         loads[2 * phase + 1].wait()
         for c in range(CHUNKS):
             cols = slice(c * HC, (c + 1) * HC)
             for j in (0, 1, 3, 2):
                 yy = lax.rem(y + j, 4)
-                if j:
+                if j and not (relayed and j == (1 if c % 2 else 3)):
                     wait_recv(piece(yy, c), h_r.at[phase, c, yy])
                 both = h[pl.ds(2 * yy, 2), h_rows, cols].reshape(2 * n, HC)
                 part = jnp.dot(both, down[cols, :], preferred_element_type=F32).reshape(2, n, FEAT)
@@ -323,7 +343,6 @@
             total += td[d - 1].astype(F32)
         return total
 
-    gain = gains[:, pl.ds(pl.multiple_of(r * FEAT, LANES), FEAT)]
     x0 = xt[...].astype(F32)
     q_rows = pl.ds(qrow, QUARTER)
     out = forward(
@@ -406,7 +425,6 @@
 
     wait_recv(gd.at[0, :, pl.ds(QUARTER, QUARTER), :], grecv.at[1], is_early)
     not_2 = g != 2
-    facing = lax.rem(y + 2, 4)
     da_2 = dab.at[1]
 
     def pass_on(c):
@@ -414,16 +432,19 @@
         passed = da_piece(da, behind, c)
         wait_recv(passed, h_r.at[2, c, behind], not_2)
         remote(passed, passed, hy_s.at[2, c, 0], h_r.at[2, c, behind], row_peer(ahead), when=not_2)
-        wait_recv(da_piece(da_2, facing, c), h_r.at[2, c, facing], is_2)
-        remote(
-            da_piece(da_2, facing, c), da_piece(da_2, facing, c), xs_s.at[c, 1], xs_r.at[c, facing], near, when=is_2
-        )
+        last = c == CHUNKS - 1
+        for j in (1, 3, 2) if last else (2,):
+            pair_2 = lax.rem(y + j, 4)
+            crossing = da_piece(da_2, pair_2, c)
+            wait_recv(crossing, h_r.at[2, c, pair_2], is_2)
+            remote(crossing, crossing, xs_s.at[c, j], xs_r.at[c, pair_2], near, when=is_2)
         wait_recv(da_piece(da_2, y, c), xs_r.at[c, y], is_3)
-        for j in (1, 3):
-            remote(
-                da_piece(da_2, y, c), da_piece(da_2, y, c), xs_s.at[c, 1 + j], xs_r.at[c, y],
-                row_peer(lax.rem(y + j, 4)), when=is_3,
-            )
+        if not last:
+            for j in (1, 3):
+                remote(
+                    da_piece(da_2, y, c), da_piece(da_2, y, c), xs_s.at[c, 3 + j], xs_r.at[c, y],
+                    row_peer(lax.rem(y + j, 4)), when=is_3,
+                )
 
     row_state = {}
 
@@ -439,7 +460,7 @@
         for j in (2, 1, 3):
             remote(
                 own_piece, own_piece, hy_s.at[2, c, j], h_r.at[2, c, y], row_peer(lax.rem(y + j, 4)),
-                when=is_2 if j == 2 else not_2,
+                when=is_2 if j == 2 else None if c == CHUNKS - 1 else not_2,
             )
         if c:
             pass_on(c - 1)
@@ -471,6 +492,14 @@
         lax.fori_loop(0, HID // step, tile, 0)
 
     n_half, n_all = BLOCKS * HALF, 2 * BLOCKS * HALF
+    outs = [pltpu.make_async_copy(gout, gen_hbm, osem.at[0]), pltpu.make_async_copy(dng_out, dng_hbm, osem.at[1])]
+    wait_recv(gout, trecv.at[3], off_diag)
+
+    @pl.when(jnp.logical_not(off_diag))
+    def _():
+        gout[...] = gen[...]
+
+    outs[0].start()
 
     @pl.when(is_2)
     def _():
@@ -493,6 +522,7 @@
             ut[:, k * LANES : (k + 1) * LANES] = two.T
         down_grad(lambda cols: hf[:, :, :, cols].reshape(n_all, -1), lambda: dyb[...].reshape(n_all, FEAT))
 
+    outs[1].start()
     for c in range(CHUNKS):
         cols = slice(c * HC, (c + 1) * HC)
         for j in (1, 3, 2):
@@ -513,21 +543,22 @@
                 ut[...], dab[:, :, :, cols].reshape(n_all, HC), preferred_element_type=F32
             ).astype(BF)
 
-    wait_recv(gout, trecv.at[3], off_diag)
-
-    @pl.when(off_diag)
-    def _():
-        gen_out[...] = gout[...].astype(F32)
-
-    @pl.when(jnp.logical_not(off_diag))
-    def _():
-        gen_out[...] = gen[...].astype(F32)
+        outs.append(pltpu.make_async_copy(upg_out.at[:, cols], upg_hbm.at[:, cols], osem.at[2 + c]))
+        outs[-1].start()
 
     for cp, when in sends:
         if when is None:
             cp.wait_send()
         else:
             pl.when(when)(cp.wait_send)
+    for cp in outs:
+        cp.wait()
+
+
+def widen(gen, up, down, gen_out, up_out, down_out):
+    gen_out[...] = gen[...]
+    up_out[0] = up[...].astype(F32)
+    down_out[0] = down[...].astype(F32)
 
 
 def rep_buffers(n):
@@ -559,13 +590,20 @@
         kernel,
         name="step",
         out_shape=(
-            jax.ShapeDtypeStruct((IMG_TOK, FEAT), F32),
+            jax.ShapeDtypeStruct((IMG_TOK, FEAT), BF),
             jax.ShapeDtypeStruct((FEAT, HID), BF),
             jax.ShapeDtypeStruct((HID, FEAT), BF),
         ),
-        in_specs=[vmem, vmem, vmem, smem, vmem, hbm, hbm],
-        out_specs=(vmem, vmem, vmem),
+        in_specs=[hbm, hbm, vmem, smem, hbm, hbm, hbm],
+        out_specs=(hbm, hbm, hbm),
         scratch_shapes=[
+            pltpu.VMEM((QUARTER, FEAT), BF),
+            pltpu.VMEM((HALF, FEAT), BF),
+            pltpu.VMEM((3, FEAT), F32),
+            pltpu.VMEM((FEAT, HID), BF),
+            pltpu.VMEM((HID, FEAT), BF),
+            dma((3,)),
+            dma((2 + CHUNKS,)),
             pltpu.VMEM((16, FEAT), BF),
             pltpu.VMEM((QUARTER, FEAT), BF),
             pltpu.VMEM((16, FEAT), BF),
@@ -611,7 +649,7 @@
             dma((3, CHUNKS, 4)),
             dma((2, 7)),
             dma((2, 7)),
-            dma((CHUNKS, 5)),
+            dma((CHUNKS, 7)),
             dma((CHUNKS, 4)),
             dma((3, 4)),
             dma((3, 4)),
@@ -624,7 +662,29 @@
             collective_id=0, has_side_effects=True, vmem_limit_bytes=60 * 2**20
         ),
     )(noise_in, noise_renoise, text_cond, t_index, gains, up_weights, down_weights)
-    return generated.astype(BF), up_grad.astype(F32)[None], down_grad.astype(F32)[None]
+    parts = 4
+    rows = [
+        pl.BlockSpec((IMG_TOK // parts, FEAT), lambda i: (i, 0)),
+        pl.BlockSpec((FEAT // parts, HID), lambda i: (i, 0)),
+        pl.BlockSpec((HID // parts, FEAT), lambda i: (i, 0)),
+    ]
+    wide = [
+        rows[0],
+        pl.BlockSpec((1, FEAT // parts, HID), lambda i: (0, i, 0)),
+        pl.BlockSpec((1, HID // parts, FEAT), lambda i: (0, i, 0)),
+    ]
+    return pl.pallas_call(
+        widen,
+        name="widen",
+        grid=(parts,),
+        out_shape=(
+            jax.ShapeDtypeStruct((IMG_TOK, FEAT), BF),
+            jax.ShapeDtypeStruct((1, FEAT, HID), F32),
+            jax.ShapeDtypeStruct((1, HID, FEAT), F32),
+        ),
+        in_specs=rows,
+        out_specs=wide,
+    )(generated, up_grad, down_grad)
 
 
 def solution(mesh):

time: 170 us -> 168 us (0.988)
  other arithmetic: 6.2 us -> 0 us
  Pallas kernels: 160 us -> 165 us
    broadcast_in_dim x2 -> x0, other arithmetic: 4.52 us -> none  [the longest x1 2.97 us: body(): up_grad.astype(F32)[None]]
    pallas_call x0 -> x1, Pallas kernels: none -> 4.38 us  [body(): pl.pallas_call(widen, name='widen', grid=(parts,), out_shape=(jax.ShapeDt...]
where the time goes in v4:
time: 168 us; the launch traced here: 167 us
  Pallas kernels  165 us (98%)
    pallas_call x1, Pallas kernels, body(): pl.pallas_call(kernel, name='step', out_shape=(jax.ShapeDtypeStruct((IMG_...  161 us
    pallas_call x1, Pallas kernels, body(): pl.pallas_call(widen, name='widen', grid=(parts,), out_shape=(jax.ShapeDt...  4.38 us

profile of v4, /device:TPU:102, one launch (start us, length us, event | category | flops | bytes accessed | tf_op | source)
XLA Modules:
  0.0 166.5 jit_solution(8916445442220447815)
XLA Ops:
  1.3 160.8 %step.1 = (bf16[128,384]{1,0:T(8,128)(2,1)}, bf16[384,1536]{1,0:T(8,128)(2,1)}, bf16[1536,384]{1,0:T(8,128)(2,1)}) custom-call(bf16[128,384]{1,0:T(8,128)(2,1)} %noise_hbm.1, bf16[128,384]{1,0:T(8,128)(2,1)} %renoise_hbm.1, bf16[1,3072]{1,0:T(2,128)(2,1)} %cond_in.1, s32[1]{0:T(128)S(6)} %copy.10.t_in, f32[3,3072]{1,0:T(4,128)} %gains_hbm.1, ...), custom_call_target="tpu_custom_call" | custom-call | tf_op jit(solution)/shard_map/step/pallas_call | solution.py:589
  162.1 4.4 %widen.1 = (bf16[128,384]{1,0:T(8,128)(2,1)}, f32[1,384,1536]{2,1,0:T(8,128)}, f32[1,1536,384]{2,1,0:T(8,128)}) custom-call(bf16[128,384]{1,0:T(8,128)(2,1)} %get-tuple-element.6.gen, bf16[384,1536]{1,0:T(8,128)(2,1)} %get-tuple-element.7.up, bf16[1536,384]{1,0:T(8,128)(2,1)} %get-tuple-element.8.down), custom_call_target="tpu_custom_call" | custom-call | tf_op jit(solution)/shard_map/widen/pallas_call | solution.py:676

commit v5 on v4

--- a/solution.py
+++ b/solution.py
@@ -56,7 +56,7 @@
     sb2, rb2, po2, zs2, zr2, acc2, ta2, tb2, tc2, td2,
     sb3, rb3, po3, zs3, zr3,
     wsem, tsend, trecv, gsend, grecv,
-    ag_s, ag_r, ry_s, ry_r, rz_s, rz_r, hy_s, h_r, tp_s, tp_r, xs_s, xs_r,
+    ag_s, ag_r, ry_s, ry_r, rz_s, rz_r, hy_s, h_r, tp_s, tp_r, xs_s, xs_r, hx_s, hx_r,
     sy_s, sy_r, sz_s, sz_r, st_s, st_r,
 ):
     g, r, t = lax.axis_index("grp"), lax.axis_index("rep"), lax.axis_index("tp")
@@ -86,6 +86,8 @@
             pl.when(when)(cp.start)
         sends.append((cp, when))
         return cp
+
+    near = dev(gg=g_near)
 
     def wait_recv(dst, rsem, when=None):
         cp = pltpu.make_async_remote_copy(
@@ -210,7 +212,7 @@
             b = 2 * lax.rem(zl + d, 4) + 1 - core
             wait_recv(sc_all.at[phase, b], st_r.at[phase, b])
 
-    def reduce_rep(phase, n, rows_of, block_of, product, bufs, finish, gathered):
+    def reduce_rep(phase, n, rows_of, block_of, product, bufs, finish, gathered, sent, after):
         sb, rb, po, zs, zr = bufs
         span = lambda c: pl.ds(c * HC, HC)
         for c in range(CHUNKS):
@@ -238,6 +240,7 @@
             if c == 0:
                 gathered()
         scalar_to_tp(phase)
+        sent()
 
         def to_z(c):
             lo = c * HC
@@ -257,15 +260,19 @@
             wait_recv(zr.at[:, span(c)], rz_r.at[phase, c])
             finish(c, po[:, lo : lo + HC] + zr[:, lo : lo + HC].astype(F32))
 
-        ahead = CHUNKS - 1 if n == HALF else CHUNKS
+        early = n == HALF
         for c in range(CHUNKS):
-            if c == ahead:
+            if early and c == CHUNKS - 1:
                 from_z(0)
             to_z(c)
-        for c in range(1 if ahead < CHUNKS else 0, CHUNKS):
+        for c in range(1 if early else 0, CHUNKS):
             from_z(c)
-
-    def forward(phase, n, x_rows, gain_row, xg, xg_rows, h, h_rows, bufs, gathered, chunk_here):
+            if c >= 2:
+                after(c - 2)
+        for c in (CHUNKS - 2, CHUNKS - 1):
+            after(c)
+
+    def forward(phase, n, x_rows, gain_row, xg, xg_rows, h, h_rows, bufs, gathered):
         acc, ta, tb, tc, td = bufs[5:]
         up, down, grad = upw.at[phase], dnw.at[phase], gd.at[phase]
         xg[t, xg_rows, :] = (x_rows * (gain_row * cond1)).astype(BF)
@@ -288,6 +295,7 @@
             passed = piece(behind, c)
             wait_recv(passed, h_r.at[phase, c, behind])
             remote(passed, passed, hy_s.at[phase, c, 2], h_r.at[phase, c, behind], row_peer(ahead))
+            remote(passed, passed, hx_s.at[c, 1 if c % 2 else 3], hx_r.at[c, behind], near, when=is_2)
 
         def finish(c, a):
             if c == 0:
@@ -302,20 +310,19 @@
                     piece(y, c), piece(y, c), hy_s.at[phase, c, j], h_r.at[phase, c, y],
                     row_peer(lax.rem(y + j, 4)),
                 )
-            if relayed and c:
-                pass_on(c - 1)
+            remote(piece(y, c), piece(y, c), hx_s.at[c, 0], hx_r.at[c, y], near, when=is_2) if relayed else None
             grad[:, h_rows, cols] = (slope * factor).astype(BF).reshape(2, n, HC)
 
-        reduce_rep(phase, n, rows_of, block_of, product, bufs[:5], finish, gathered)
-        if relayed:
-            pass_on(CHUNKS - 1)
-        loads[2 * phase + 1].wait()
-        for c in range(CHUNKS):
+        def project(c):
+            if c == 0:
+                loads[2 * phase + 1].wait()
             cols = slice(c * HC, (c + 1) * HC)
             for j in (0, 1, 3, 2):
                 yy = lax.rem(y + j, 4)
                 if j and not (relayed and j == (1 if c % 2 else 3)):
                     wait_recv(piece(yy, c), h_r.at[phase, c, yy])
+                    if relayed:
+                        remote(piece(yy, c), piece(yy, c), hx_s.at[c, j], hx_r.at[c, yy], near, when=is_2)
                 both = h[pl.ds(2 * yy, 2), h_rows, cols].reshape(2 * n, HC)
                 part = jnp.dot(both, down[cols, :], preferred_element_type=F32).reshape(2, n, FEAT)
                 if c:
@@ -324,7 +331,16 @@
                 if c == CHUNKS - 1:
                     ta[yy] = acc[2 * yy + 1 - core].astype(BF)
                     remote(ta.at[yy], tb.at[yy], tp_s.at[phase, yy], tp_r.at[phase, yy], sibling)
-            chunk_here(c)
+
+        def after(c):
+            if relayed:
+                pass_on(c)
+                if c:
+                    project(c - 1)
+
+        reduce_rep(phase, n, rows_of, block_of, product, bufs[:5], finish, gathered, lambda: None, after)
+        for c in range(CHUNKS - 1 if relayed else 0, CHUNKS):
+            project(c)
         total = None
         for d in (2, 1, 3, 0):
             yy = lax.rem(zl + d, 4)
@@ -347,7 +363,7 @@
     q_rows = pl.ds(qrow, QUARTER)
     out = forward(
         0, QUARTER, x0, gain[0:1, :], xgs, q_rows, hs, q_rows,
-        (sb1, rb1, po1, zs1, zr1, acc1, ta1, tb1, tc1, td1), lambda: None, lambda c: None,
+        (sb1, rb1, po1, zs1, zr1, acc1, ta1, tb1, tc1, td1), lambda: None,
     )
     gen[own, :] = (x0 + out).astype(BF)
     remote(gen.at[own, :], gen.at[own, :], gsend.at[0], grecv.at[0], dev(gg=g_pair))
@@ -363,8 +379,6 @@
     x_t = ((1.0 - sigma) * gen_f + sigma * rt[...].astype(F32)).astype(BF).astype(F32)
     all_rows = pl.ds(0, HALF)
     xgf_2 = xgf.at[1]
-    hf_2 = lambda c: hf.at[1, :, :, pl.ds(c * HC, HC)]
-    near = dev(gg=g_near)
 
     def inputs_here():
         wait_recv(gen.at[other, :], grecv.at[4])
@@ -376,7 +390,6 @@
         1, HALF, x_t, gain_row, xgf.at[half], all_rows, hf.at[half], all_rows,
         (sb2, rb2, po2, zs2, zr2, acc2, ta2, tb2, tc2, td2),
         inputs_here,
-        lambda c: remote(hf_2(c), hf_2(c), gsend.at[10 + c], grecv.at[10 + c], near, when=is_2),
     )
     fk[...] = (x_t + out).astype(BF)
     remote(fk, fother, gsend.at[6], grecv.at[6], dev(gg=g_pair), when=is_late)
@@ -462,66 +475,86 @@
                 own_piece, own_piece, hy_s.at[2, c, j], h_r.at[2, c, y], row_peer(lax.rem(y + j, 4)),
                 when=is_2 if j == 2 else None if c == CHUNKS - 1 else not_2,
             )
-        if c:
-            pass_on(c - 1)
 
     dyb_2 = dyb.at[1]
+    n_half, n_all = BLOCKS * HALF, 2 * BLOCKS * HALF
+
+    def turned():
+        @pl.when(is_early)
+        def _():
+            wait_recv(xgs_other, grecv.at[2])
+            for k in range(BLOCKS // 2):
+                two = xgs[2 * k : 2 * k + 2].reshape(2 * HALF, FEAT)
+                ut[:, k * LANES : (k + 1) * LANES] = two.T
+
+        @pl.when(is_3)
+        def _():
+            wait_recv(xgf_2, grecv.at[5])
+            for k in range(BLOCKS):
+                two = xgf[k // 4, 2 * (k % 4) : 2 * (k % 4) + 2].reshape(2 * HALF, FEAT)
+                ut[:, k * LANES : (k + 1) * LANES] = two.T
+
+    tn = (((0,), (0,)), ((), ()))
+    step = 256
+
+    def down_tiles(first, last):
+        for i in range(first, last):
+            cols = slice(i * step, (i + 1) * step)
+
+            @pl.when(is_early)
+            def _():
+                dng_out[cols, :] = lax.dot_general(
+                    hs[:, :, cols].reshape(n_half, step), dys[...].reshape(n_half, FEAT), tn,
+                    preferred_element_type=F32,
+                ).astype(BF)
+
+            @pl.when(is_3)
+            def _():
+                dng_out[cols, :] = lax.dot_general(
+                    hf[:, :, :, cols].reshape(n_all, step), dyb[...].reshape(n_all, FEAT), tn,
+                    preferred_element_type=F32,
+                ).astype(BF)
+
+    def after(c):
+        pass_on(c)
+        if c == 0:
+
+            @pl.when(is_early)
+            def _():
+                wait_recv(hs_other, grecv.at[3])
+                for b in range(BLOCKS):
+                    dys[b] = (dy[b].astype(F32) * image_scale(b)).astype(BF)
+
+            @pl.when(is_3)
+            def _():
+                for k in range(CHUNKS):
+                    for yy in range(4):
+                        wait_recv(hf.at[1, 2 * yy : 2 * yy + 2, :, pl.ds(k * HC, HC)], hx_r.at[k, yy])
+                wait_recv(dyb_2, grecv.at[8])
+
+        if c < 3:
+            down_tiles(2 * c, 2 * c + 2)
+
+    xgs_other, hs_other = xgs.at[:, pl.ds(QUARTER, QUARTER), :], hs.at[:, pl.ds(QUARTER, QUARTER), :]
     reduce_rep(
         2, HALF, lambda yy: dy[pl.ds(2 * yy, 2)].reshape(2 * HALF, FEAT), dy_block, product,
         (sb3, rb3, po3, zs3, zr3), finish,
-        lambda: remote(dyb_2, dyb_2, gsend.at[8], grecv.at[8], near, when=is_2),
+        lambda: remote(dyb_2, dyb_2, gsend.at[8], grecv.at[8], near, when=is_2), turned, after,
     )
-    pass_on(CHUNKS - 1)
-
-    for i, ref in enumerate((xgs.at[:, pl.ds(QUARTER, QUARTER), :], hs.at[:, pl.ds(QUARTER, QUARTER), :])):
-        wait_recv(ref, grecv.at[2 + i], is_early)
-    wait_recv(xgf_2, grecv.at[5], is_3)
-    for c in range(CHUNKS):
-        wait_recv(hf_2(c), grecv.at[10 + c], is_3)
-    wait_recv(dyb_2, grecv.at[8], is_3)
-
-    tn = (((0,), (0,)), ((), ()))
-    step = 256
-
-    def down_grad(h_of, upstream_of):
-        def tile(i, _):
-            cols = pl.ds(pl.multiple_of(i * step, step), step)
-            dng_out[cols, :] = lax.dot_general(h_of(cols), upstream_of(), tn, preferred_element_type=F32).astype(BF)
-            return 0
-
-        lax.fori_loop(0, HID // step, tile, 0)
-
-    n_half, n_all = BLOCKS * HALF, 2 * BLOCKS * HALF
+
     outs = [pltpu.make_async_copy(gout, gen_hbm, osem.at[0]), pltpu.make_async_copy(dng_out, dng_hbm, osem.at[1])]
     wait_recv(gout, trecv.at[3], off_diag)
 
     @pl.when(jnp.logical_not(off_diag))
     def _():
         gout[...] = gen[...]
-
-    outs[0].start()
 
     @pl.when(is_2)
     def _():
         upg_out[...] = jnp.zeros_like(upg_out)
         dng_out[...] = jnp.zeros_like(dng_out)
 
-    @pl.when(is_early)
-    def _():
-        for k in range(BLOCKS // 2):
-            two = xgs[2 * k : 2 * k + 2].reshape(2 * HALF, FEAT)
-            ut[:, k * LANES : (k + 1) * LANES] = two.T
-        for b in range(BLOCKS):
-            dys[b] = (dy[b].astype(F32) * image_scale(b)).astype(BF)
-        down_grad(lambda cols: hs[:, :, cols].reshape(n_half, -1), lambda: dys[...].reshape(n_half, FEAT))
-
-    @pl.when(is_3)
-    def _():
-        for k in range(BLOCKS):
-            two = xgf[k // 4, 2 * (k % 4) : 2 * (k % 4) + 2].reshape(2 * HALF, FEAT)
-            ut[:, k * LANES : (k + 1) * LANES] = two.T
-        down_grad(lambda cols: hf[:, :, :, cols].reshape(n_all, -1), lambda: dyb[...].reshape(n_all, FEAT))
-
+    outs[0].start()
     outs[1].start()
     for c in range(CHUNKS):
         cols = slice(c * HC, (c + 1) * HC)
@@ -637,8 +670,8 @@
             dma((4,)),
             dma((4,)),
             dma((4,)),
-            dma((10 + CHUNKS,)),
-            dma((10 + CHUNKS,)),
+            dma((10,)),
+            dma((10,)),
             dma((3, 7)),
             dma((3, 8)),
             dma((3, CHUNKS, 4)),
@@ -650,6 +683,8 @@
             dma((2, 7)),
             dma((2, 7)),
             dma((CHUNKS, 7)),
+            dma((CHUNKS, 4)),
+            dma((CHUNKS, 4)),
             dma((CHUNKS, 4)),
             dma((3, 4)),
             dma((3, 4)),

time: 168 us -> 170 us (1.012)
  Pallas kernels: 165 us -> 168 us
    pallas_call x1, Pallas kernels: 161 us -> 164 us  [body(): pl.pallas_call(kernel, name='step', out_shape=(jax.ShapeDtypeStruct((IMG_...]
where the time goes in v5:
time: 170 us; the launch traced here: 169 us
  Pallas kernels  168 us (99%)
    pallas_call x1, Pallas kernels, body(): pl.pallas_call(kernel, name='step', out_shape=(jax.ShapeDtypeStruct((IMG_...  164 us
    pallas_call x1, Pallas kernels, body(): pl.pallas_call(widen, name='widen', grid=(parts,), out_shape=(jax.ShapeDt...  4.38 us

profile of v5, /device:TPU:102, one launch (start us, length us, event | category | flops | bytes accessed | tf_op | source)
XLA Modules:
  0.0 169.5 jit_solution(7636733213351906893)
XLA Ops:
  1.3 163.8 %step.1 = (bf16[128,384]{1,0:T(8,128)(2,1)}, bf16[384,1536]{1,0:T(8,128)(2,1)}, bf16[1536,384]{1,0:T(8,128)(2,1)}) custom-call(bf16[128,384]{1,0:T(8,128)(2,1)} %noise_hbm.1, bf16[128,384]{1,0:T(8,128)(2,1)} %renoise_hbm.1, bf16[1,3072]{1,0:T(2,128)(2,1)} %cond_in.1, s32[1]{0:T(128)S(6)} %copy.10.t_in, f32[3,3072]{1,0:T(4,128)} %gains_hbm.1, ...), custom_call_target="tpu_custom_call" | custom-call | tf_op jit(solution)/shard_map/step/pallas_call | solution.py:622
  165.1 4.4 %widen.1 = (bf16[128,384]{1,0:T(8,128)(2,1)}, f32[1,384,1536]{2,1,0:T(8,128)}, f32[1,1536,384]{2,1,0:T(8,128)}) custom-call(bf16[128,384]{1,0:T(8,128)(2,1)} %get-tuple-element.6.gen, bf16[384,1536]{1,0:T(8,128)(2,1)} %get-tuple-element.7.up, bf16[1536,384]{1,0:T(8,128)(2,1)} %get-tuple-element.8.down), custom_call_target="tpu_custom_call" | custom-call | tf_op jit(solution)/shard_map/widen/pallas_call | solution.py:711

commit v6 on v5

--- a/solution.py
+++ b/solution.py
@@ -14,7 +14,7 @@
 FEAT = 384
 HID = 1536
 LANES = 128
-CHUNKS = 4
+CHUNKS = 6
 HC = HID // CHUNKS
 BLOCKS = 8
 HALF = 64
@@ -289,6 +289,7 @@
 
         state = {}
         relayed = n == HALF
+        passing = lambda c: relayed and c < CHUNKS - 2
 
         def pass_on(c):
             behind, ahead = lax.rem(y + (1 if c % 2 else 3), 4), lax.rem(y + (3 if c % 2 else 1), 4)
@@ -305,7 +306,7 @@
             hidden, slope = gelu_both(a * factor)
             cols = slice(c * HC, (c + 1) * HC)
             h[pl.ds(2 * y, 2), h_rows, cols] = hidden.astype(BF).reshape(2, n, HC)
-            for j in (1, 3) if relayed else (2, 1, 3):
+            for j in (1, 3) if passing(c) else (2, 1, 3):
                 remote(
                     piece(y, c), piece(y, c), hy_s.at[phase, c, j], h_r.at[phase, c, y],
                     row_peer(lax.rem(y + j, 4)),
@@ -319,7 +320,7 @@
             cols = slice(c * HC, (c + 1) * HC)
             for j in (0, 1, 3, 2):
                 yy = lax.rem(y + j, 4)
-                if j and not (relayed and j == (1 if c % 2 else 3)):
+                if j and not (passing(c) and j == (1 if c % 2 else 3)):
                     wait_recv(piece(yy, c), h_r.at[phase, c, yy])
                     if relayed:
                         remote(piece(yy, c), piece(yy, c), hx_s.at[c, j], hx_r.at[c, yy], near, when=is_2)
@@ -333,13 +334,13 @@
                     remote(ta.at[yy], tb.at[yy], tp_s.at[phase, yy], tp_r.at[phase, yy], sibling)
 
         def after(c):
-            if relayed:
+            if passing(c):
                 pass_on(c)
-                if c:
-                    project(c - 1)
+            if relayed and c >= 3:
+                project(c - 3)
 
         reduce_rep(phase, n, rows_of, block_of, product, bufs[:5], finish, gathered, lambda: None, after)
-        for c in range(CHUNKS - 1 if relayed else 0, CHUNKS):
+        for c in range(CHUNKS - 3 if relayed else 0, CHUNKS):
             project(c)
         total = None
         for d in (2, 1, 3, 0):
@@ -443,9 +444,10 @@
     def pass_on(c):
         behind, ahead = lax.rem(y + (1 if c % 2 else 3), 4), lax.rem(y + (3 if c % 2 else 1), 4)
         passed = da_piece(da, behind, c)
-        wait_recv(passed, h_r.at[2, c, behind], not_2)
-        remote(passed, passed, hy_s.at[2, c, 0], h_r.at[2, c, behind], row_peer(ahead), when=not_2)
-        last = c == CHUNKS - 1
+        if c < CHUNKS - 1:
+            wait_recv(passed, h_r.at[2, c, behind], not_2)
+            remote(passed, passed, hy_s.at[2, c, 0], h_r.at[2, c, behind], row_peer(ahead), when=not_2)
+        last = c >= CHUNKS - 2
         for j in (1, 3, 2) if last else (2,):
             pair_2 = lax.rem(y + j, 4)
             crossing = da_piece(da_2, pair_2, c)
@@ -459,6 +461,11 @@
                     row_peer(lax.rem(y + j, 4)), when=is_3,
                 )
 
+    def when_sent(c, j):
+        if j == 2:
+            return None if c == CHUNKS - 1 else is_2
+        return None if c >= CHUNKS - 2 else not_2
+
     row_state = {}
 
     def finish(c, dh):
@@ -473,7 +480,7 @@
         for j in (2, 1, 3):
             remote(
                 own_piece, own_piece, hy_s.at[2, c, j], h_r.at[2, c, y], row_peer(lax.rem(y + j, 4)),
-                when=is_2 if j == 2 else None if c == CHUNKS - 1 else not_2,
+                when=when_sent(c, j),
             )
 
     dyb_2 = dyb.at[1]
@@ -560,7 +567,7 @@
         cols = slice(c * HC, (c + 1) * HC)
         for j in (1, 3, 2):
             yy = lax.rem(y + j, 4)
-            if j != (1 if c % 2 else 3):
+            if c == CHUNKS - 1 or j != (1 if c % 2 else 3):
                 wait_recv(da_piece(da, yy, c), h_r.at[2, c, yy], not_2)
             wait_recv(da_piece(da_2, yy, c), xs_r.at[c, yy], is_3)
 

time: 170 us -> 171 us (level)
  the two profiles are of different devices: /device:TPU:102 before, /device:TPU:71 now
where the time goes in v6:
time: 171 us
  Pallas kernels  169 us (99%)
    pallas_call x1, Pallas kernels, body(): pl.pallas_call(kernel, name='step', out_shape=(jax.ShapeDtypeStruct((IMG_...  165 us
    pallas_call x1, Pallas kernels, body(): pl.pallas_call(widen, name='widen', grid=(parts,), out_shape=(jax.ShapeDt...  4.38 us

profile of v6, /device:TPU:71, one launch (start us, length us, event | category | flops | bytes accessed | tf_op | source)
XLA Modules:
  0.0 170.7 jit_solution(3778158661384603900)
XLA Ops:
  1.3 165.0 %step.1 = (bf16[128,384]{1,0:T(8,128)(2,1)}, bf16[384,1536]{1,0:T(8,128)(2,1)}, bf16[1536,384]{1,0:T(8,128)(2,1)}) custom-call(bf16[128,384]{1,0:T(8,128)(2,1)} %noise_hbm.1, bf16[128,384]{1,0:T(8,128)(2,1)} %renoise_hbm.1, bf16[1,3072]{1,0:T(2,128)(2,1)} %cond_in.1, s32[1]{0:T(128)S(6)} %copy.10.t_in, f32[3,3072]{1,0:T(4,128)} %gains_hbm.1, ...), custom_call_target="tpu_custom_call" | custom-call | tf_op jit(solution)/shard_map/step/pallas_call | solution.py:629
  166.3 4.4 %widen.1 = (bf16[128,384]{1,0:T(8,128)(2,1)}, f32[1,384,1536]{2,1,0:T(8,128)}, f32[1,1536,384]{2,1,0:T(8,128)}) custom-call(bf16[128,384]{1,0:T(8,128)(2,1)} %get-tuple-element.6.gen, bf16[384,1536]{1,0:T(8,128)(2,1)} %get-tuple-element.7.up, bf16[1536,384]{1,0:T(8,128)(2,1)} %get-tuple-element.8.down), custom_call_target="tpu_custom_call" | custom-call | tf_op jit(solution)/shard_map/widen/pallas_call | solution.py:718

commit v7 on v6

--- a/solution.py
+++ b/solution.py
@@ -14,7 +14,7 @@
 FEAT = 384
 HID = 1536
 LANES = 128
-CHUNKS = 6
+CHUNKS = 4
 HC = HID // CHUNKS
 BLOCKS = 8
 HALF = 64
@@ -168,13 +168,15 @@
             to = dev(tt=2 * lax.rem(zl + d, 4) + core)
             remote(block_of(t), block_of(t), ag_s.at[phase, d], ag_r.at[phase, t], to)
 
+    def wait_link(phase, block_of, d):
+        b = 2 * lax.rem(zl + d, 4) + core
+        wait_recv(block_of(b), ag_r.at[phase, b])
+        remote(block_of(b), block_of(b), ag_s.at[phase, 3 + d], ag_r.at[phase, b], sibling)
+
     def wait_chip(phase, block_of, d):
-        yy = lax.rem(zl + d, 4)
-        if d:
-            b = 2 * yy + core
-            wait_recv(block_of(b), ag_r.at[phase, b])
-            remote(block_of(b), block_of(b), ag_s.at[phase, 3 + d], ag_r.at[phase, b], sibling)
-        b = 2 * yy + 1 - core
+        for nearest in {1: (1, 3), 3: (2,)}.get(d, ()):
+            wait_link(phase, block_of, nearest)
+        b = 2 * lax.rem(zl + d, 4) + 1 - core
         wait_recv(block_of(b), ag_r.at[phase, b])
 
     def scalar_start(phase, lanes):
@@ -447,7 +449,7 @@
         if c < CHUNKS - 1:
             wait_recv(passed, h_r.at[2, c, behind], not_2)
             remote(passed, passed, hy_s.at[2, c, 0], h_r.at[2, c, behind], row_peer(ahead), when=not_2)
-        last = c >= CHUNKS - 2
+        last = c == CHUNKS - 1
         for j in (1, 3, 2) if last else (2,):
             pair_2 = lax.rem(y + j, 4)
             crossing = da_piece(da_2, pair_2, c)
@@ -464,7 +466,7 @@
     def when_sent(c, j):
         if j == 2:
             return None if c == CHUNKS - 1 else is_2
-        return None if c >= CHUNKS - 2 else not_2
+        return None if c == CHUNKS - 1 else not_2
 
     row_state = {}
 

time: 171 us -> 167 us (0.977)
  the two profiles are of different devices: /device:TPU:71 before, /device:TPU:102 now
where the time goes in v7:
time: 167 us; the launch traced here: 164 us
  Pallas kernels  163 us (98%)
    pallas_call x1, Pallas kernels, body(): pl.pallas_call(kernel, name='step', out_shape=(jax.ShapeDtypeStruct((IMG_...  158 us
    pallas_call x1, Pallas kernels, body(): pl.pallas_call(widen, name='widen', grid=(parts,), out_shape=(jax.ShapeDt...  4.38 us

profile of v7, /device:TPU:102, one launch (start us, length us, event | category | flops | bytes accessed | tf_op | source)
XLA Modules:
  0.0 163.8 jit_solution(8409963497726316676)
XLA Ops:
  1.3 158.1 %step.1 = (bf16[128,384]{1,0:T(8,128)(2,1)}, bf16[384,1536]{1,0:T(8,128)(2,1)}, bf16[1536,384]{1,0:T(8,128)(2,1)}) custom-call(bf16[128,384]{1,0:T(8,128)(2,1)} %noise_hbm.1, bf16[128,384]{1,0:T(8,128)(2,1)} %renoise_hbm.1, bf16[1,3072]{1,0:T(2,128)(2,1)} %cond_in.1, s32[1]{0:T(128)S(6)} %copy.10.t_in, f32[3,3072]{1,0:T(4,128)} %gains_hbm.1, ...), custom_call_target="tpu_custom_call" | custom-call | tf_op jit(solution)/shard_map/step/pallas_call | solution.py:631
  159.4 4.4 %widen.1 = (bf16[128,384]{1,0:T(8,128)(2,1)}, f32[1,384,1536]{2,1,0:T(8,128)}, f32[1,1536,384]{2,1,0:T(8,128)}) custom-call(bf16[128,384]{1,0:T(8,128)(2,1)} %get-tuple-element.6.gen, bf16[384,1536]{1,0:T(8,128)(2,1)} %get-tuple-element.7.up, bf16[1536,384]{1,0:T(8,128)(2,1)} %get-tuple-element.8.down), custom_call_target="tpu_custom_call" | custom-call | tf_op jit(solution)/shard_map/widen/pallas_call | solution.py:720

commit v8 on v7

--- a/solution.py
+++ b/solution.py
@@ -706,7 +706,7 @@
             collective_id=0, has_side_effects=True, vmem_limit_bytes=60 * 2**20
         ),
     )(noise_in, noise_renoise, text_cond, t_index, gains, up_weights, down_weights)
-    parts = 4
+    parts = 2
     rows = [
         pl.BlockSpec((IMG_TOK // parts, FEAT), lambda i: (i, 0)),
         pl.BlockSpec((FEAT // parts, HID), lambda i: (i, 0)),

time: 167 us -> 166 us (level)
  no operation moved by 1% of the time
where the time goes in v8:
time: 166 us; the launch traced here: 163 us
  Pallas kernels  162 us (98%)
    pallas_call x1, Pallas kernels, body(): pl.pallas_call(kernel, name='step', out_shape=(jax.ShapeDtypeStruct((IMG_...  158 us
    pallas_call x1, Pallas kernels, body(): pl.pallas_call(widen, name='widen', grid=(parts,), out_shape=(jax.ShapeDt...  3.6 us

profile of v8, /device:TPU:102, one launch (start us, length us, event | category | flops | bytes accessed | tf_op | source)
XLA Modules:
  0.0 163.0 jit_solution(7545530993526653029)
XLA Ops:
  1.3 158.1 %step.1 = (bf16[128,384]{1,0:T(8,128)(2,1)}, bf16[384,1536]{1,0:T(8,128)(2,1)}, bf16[1536,384]{1,0:T(8,128)(2,1)}) custom-call(bf16[128,384]{1,0:T(8,128)(2,1)} %noise_hbm.1, bf16[128,384]{1,0:T(8,128)(2,1)} %renoise_hbm.1, bf16[1,3072]{1,0:T(2,128)(2,1)} %cond_in.1, s32[1]{0:T(128)S(6)} %copy.10.t_in, f32[3,3072]{1,0:T(4,128)} %gains_hbm.1, ...), custom_call_target="tpu_custom_call" | custom-call | tf_op jit(solution)/shard_map/step/pallas_call | solution.py:631
  159.4 3.6 %widen.1 = (bf16[128,384]{1,0:T(8,128)(2,1)}, f32[1,384,1536]{2,1,0:T(8,128)}, f32[1,1536,384]{2,1,0:T(8,128)}) custom-call(bf16[128,384]{1,0:T(8,128)(2,1)} %get-tuple-element.6.gen, bf16[384,1536]{1,0:T(8,128)(2,1)} %get-tuple-element.7.up, bf16[1536,384]{1,0:T(8,128)(2,1)} %get-tuple-element.8.down), custom_call_target="tpu_custom_call" | custom-call | tf_op jit(solution)/shard_map/widen/pallas_call | solution.py:720
